TPU v7x, 32 devices: a whole 2x2x4 slice. The times are simulated.
32 devices in a mesh: ep: 4 (over y, x), edp: 4 (over z), tp: 2 (over core).
Axes of the slice: x: 2, y: 2, z: 4, core: 2. Of those that a mesh axis runs over, the one named last changes fastest.
Arguments:
- tokens: bfloat16 [2048, 4096], P(('ep', 'edp'), 'tp'), may hold values from -6 to 6
- cotangent: bfloat16 [2048, 4096], P(('ep', 'edp'), 'tp'), may hold values from -6 to 6
- expert_ids: int32 [2048, 8], P(('ep', 'edp')), may hold values from 0 to 127, all different within a row; in each aligned block of 128 rows (0 to 127, 128 to 255, ...) at most 10 rows name the same one
- route_weights: float32 [2048, 8], P(('ep', 'edp')), may hold values from 0.1 to 1
- expert_weights: bfloat16 [3, 1536, 4096], P(None, ('ep', 'tp')), may hold values from -0.15625 to 0.15625
Outputs:
- mixed: bfloat16 [2048, 4096], P(('ep', 'edp'), 'tp')
- grad_tokens: bfloat16 [2048, 4096], P(('ep', 'edp'), 'tp')
- weight_grads: float32 [3, 1536, 4096], P(None, ('ep', 'tp'), 'edp')
Inputs may be any that keep to these rules, and one draw needn't show every extreme that they name: `expert_ids`: each token names 8 different experts; within the tokens of one (ep, edp) index no expert is named by more than 10 tokens.
All inputs are finite; a program needn't handle non-finite values.
Results may differ from a plain program's by a relative error of at most 0.017.
Values may be sent and summed in bfloat16 or wider, within the bound.
A program may use at most 64 MiB of HBM per device.

v0:
```python
import functools

import jax
import jax.numpy as jnp
import numpy as np
from jax import lax
from jax.experimental import pallas as pl
from jax.experimental.pallas import tpu as pltpu
from jax.sharding import PartitionSpec as P

CAP = 10
PARTS = 4
VMEM_LIMIT = 61 * 1024 * 1024
MESH = pl.DeviceIdType.MESH
F32 = jnp.float32
BF16 = jnp.bfloat16


def round_up(value, unit):
    return -(-value // unit) * unit


class Sizes:
    def __init__(self, ep, edp, tp, tok_rows, feats, hid):
        self.ep, self.edp, self.tp = ep, edp, tp
        self.window = ep // PARTS
        self.tok_rows, self.feats, self.hid = tok_rows, feats, hid
        self.block = feats * tp // edp
        self.nblk = feats // self.block
        self.nch = max(1, min(4, self.block // 128))
        self.cw = self.block // self.nch
        self.xr = round_up(2 * CAP * self.nch, 16)
        self.rows = round_up(ep * CAP, 16)
        self.lanes = round_up(3 * ep * CAP, 128)


def permutations(z):
    table = np.zeros((z.nch, 2, z.rows, z.ep, z.xr), np.float32)
    factor = np.zeros((z.nch, z.lanes, z.ep, z.xr), np.float32)
    place = np.zeros((3, z.rows, z.lanes), np.float32)
    for i in range(z.ep):
        for c in range(CAP):
            for q in range(z.nch):
                for a in range(2):
                    table[q, a, i * CAP + c, i, (2 * q + a) * CAP + c] = 1.0
                for m in range(3):
                    factor[q, (m * z.ep + i) * CAP + c, i, (2 * q + m // 2) * CAP + c] = 1.0
            for m in range(3):
                place[m, i * CAP + c, (m * z.ep + i) * CAP + c] = 1.0
    flat = table.reshape(z.nch, 2 * z.rows, z.ep * z.xr)
    return (
        flat.reshape(-1, z.ep * z.xr), np.swapaxes(flat, 1, 2).copy(),
        factor.reshape(-1, z.ep * z.xr), place,
    )


def slot_parts(index, nch):
    chunk = jnp.zeros_like(index)
    for k in range(1, nch):
        chunk += (index >= 2 * CAP * k).astype(jnp.int32)
    rest = index - 2 * CAP * chunk
    array = (rest >= CAP).astype(jnp.int32)
    return chunk, array, rest - CAP * array


def kernel(
    z, tok_in, cot_in, ids_in, rw_in, perm_in, perm_t_in, factor_in, place_in, weights,
    left, right_out, summed_out, homes_out,
    tok, cot, ids, rw, perm, perm_t, factor, place,
    wb, x, xin, rb, rows, pout, pin, hb, lout, lb, ob, y, yin, right, summed, homes,
    out_sem, in_sem, w_loc, w_send, w_recv, x_send, x_recv, r_send, r_recv, p_send, p_recv,
    l_send, l_recv, y_send, y_recv, q_send, q_recv,
):
    i, e, s = lax.axis_index("ep"), lax.axis_index("edp"), lax.axis_index("tp")
    barrier = pltpu.get_barrier_semaphore()
    group = z.ep * z.edp

    loads = [
        pltpu.make_async_copy(source, target, in_sem.at[k])
        for k, (source, target) in enumerate((
            (ids_in, ids), (rw_in, rw), (tok_in, tok), (cot_in, cot),
            (perm_in, perm), (perm_t_in, perm_t), (factor_in, factor), (place_in, place),
        ))
    ]
    for copy in loads[:4]:
        copy.start()

    def greet(step, carry):
        di = step // z.edp
        de = step - di * z.edp
        pl.semaphore_signal(
            barrier, inc=1,
            device_id=(lax.rem(i + di, z.ep), lax.rem(e + de, z.edp), s),
            device_id_type=MESH,
        )
        return carry

    for d in range(1, z.tp):
        pl.semaphore_signal(
            barrier, inc=1, device_id=(i, e, lax.rem(s + d, z.tp)), device_id_type=MESH
        )
    lax.fori_loop(1, group, greet, 0)

    own_w = pltpu.make_async_copy(
        weights.at[:, :, pl.ds(pl.multiple_of(s * z.feats, 128), z.feats)], wb.at[s], w_loc
    )
    own_w.start()
    for copy in loads[4:]:
        copy.start()

    row = lax.broadcasted_iota(jnp.int32, (z.xr, z.tok_rows), 0)
    chunk, array, slot = slot_parts(row, z.nch)
    in_use = row < 2 * CAP * z.nch
    before = (
        lax.broadcasted_iota(jnp.int32, (z.tok_rows, z.tok_rows), 0)
        < lax.broadcasted_iota(jnp.int32, (z.tok_rows, z.tok_rows), 1)
    ).astype(F32).astype(BF16)
    lane = lax.broadcasted_iota(jnp.int32, (z.tok_rows, z.xr), 1)
    lane_chunk, lane_array, _ = slot_parts(lane, z.nch)
    loads[0].wait()
    loads[1].wait()
    ids_t = ids[...]
    rw_t = rw[...]
    chosen, scales, picks = [], [], []
    for w in range(z.window):
        hit = (ids_t == w).astype(F32)
        match = jnp.sum(hit, axis=0, keepdims=True)
        weight = jnp.sum(hit * rw_t, axis=0, keepdims=True)
        match_all = jnp.broadcast_to(match, (z.xr, z.tok_rows))
        rank = jnp.dot(match_all.astype(BF16), before, preferred_element_type=F32)
        pick = jnp.where(in_use & (rank == slot.astype(F32)), match_all, 0.0)
        slot_weight = jnp.sum(pick * weight, axis=1, keepdims=True)
        picks.append(pick)
        scales.append((
            jnp.where(array[:, :1] == 1, slot_weight, 1.0), jnp.where(array[:, :1] == 0, slot_weight, 1.0),
        ))
        chosen.append([
            [jnp.where((chunk == q) & (array == a), pick, 0.0).astype(BF16) for a in range(2)]
            for q in range(z.nch)
        ])
    pl.semaphore_wait(barrier, group - 1 + z.tp - 1)

    sent = []
    for b in range(z.nblk):
        for d in range(1, z.tp):
            to = lax.rem(s + d, z.tp)
            cols = pl.ds(pl.multiple_of(to * z.feats + b * z.block, 128), z.block)
            sent.append(pltpu.make_async_remote_copy(
                src_ref=weights.at[:, :, cols],
                dst_ref=wb.at[s, :, :, pl.ds(b * z.block, z.block)],
                send_sem=w_send.at[d * z.nblk + b], recv_sem=w_recv.at[s * z.nblk + b],
                device_id=(i, e, to), device_id_type=MESH,
            ))
            sent[-1].start()
    loads[2].wait()
    loads[3].wait()
    for b in range(z.nblk):
        for w in range(z.window):
            total = jnp.zeros((z.xr, z.cw), F32)
            for q in range(z.nch):
                cols = pl.ds(b * z.block + q * z.cw, z.cw)
                for a, source in ((0, tok), (1, cot)):
                    total += jnp.dot(chosen[w][q][a], source[:, cols], preferred_element_type=F32)
            x[w, b] = (total * scales[w][0]).astype(BF16)
        for d in range(1, z.ep):
            to = lax.rem(i + d, z.ep)
            sent.append(pltpu.make_async_remote_copy(
                src_ref=x.at[to // PARTS, b], dst_ref=xin.at[i, b],
                send_sem=x_send.at[d * z.nblk + b], recv_sem=x_recv.at[i * z.nblk + b],
                device_id=(to, e, s), device_id_type=MESH,
            ))
            sent[-1].start()

    def right_copy(b, d):
        to = lax.rem(i + d, z.ep)
        return pltpu.make_async_remote_copy(
            src_ref=x.at[to // PARTS, b], dst_ref=rb.at[e, i],
            send_sem=r_send.at[b * z.ep + d], recv_sem=r_recv.at[0],
            device_id=(to, s * z.nblk + b, s), device_id_type=MESH,
        )

    for b in range(z.nblk):
        @pl.when(s * z.nblk + b != e)
        def _():
            for d in range(z.ep):
                right_copy(b, d).start()

    xin[i] = x[i // PARTS]
    for w in range(z.window):
        home = jnp.transpose(picks[w])
        for q in range(z.nch):
            for a in range(2):
                homes[w, 2 * q + a] = jnp.where(
                    (lane_chunk == q) & (lane_array == a), home, 0.0
                ).astype(BF16)
    own_w.wait()
    for copy in loads[4:]:
        copy.wait()

    last = (((1,), (1,)), ((), ()))
    for b in range(z.nblk):
        for d in range(1, z.ep):
            source = lax.rem(i + d, z.ep)
            landed = xin.at[source, b]
            pltpu.make_async_copy(landed, landed, x_recv.at[source * z.nblk + b]).wait()
        flat = jnp.dot(
            perm[...], xin[:, b].reshape(z.ep * z.xr, z.cw), preferred_element_type=F32
        ).astype(BF16)
        block = pl.ds(b * z.block, z.block)
        for q in range(z.nch):
            cols = pl.ds(b * z.block + q * z.cw, z.cw)
            rows[:, cols] = flat[q * 2 * z.rows:(q + 1) * 2 * z.rows]
        for d in range(1, z.tp):
            source = lax.rem(s + d, z.tp)
            landed = wb.at[source, :, :, block]
            pltpu.make_async_copy(landed, landed, w_recv.at[source * z.nblk + b]).wait()
        for m in range(3):
            part = rows[:z.rows, block] if m < 2 else rows[z.rows:, block]
            for t in range(z.tp):
                value = lax.dot_general(part, wb[t, m, :, block], last, preferred_element_type=F32)
                if b:
                    value += pout[m, t]
                pout[m, t] = value
            if b == z.nblk - 1:
                for d in range(1, z.tp):
                    sent.append(pltpu.make_async_remote_copy(
                        src_ref=pout.at[m], dst_ref=pin.at[s, m],
                        send_sem=p_send.at[d * 3 + m], recv_sem=p_recv.at[s * 3 + m],
                        device_id=(i, e, lax.rem(s + d, z.tp)), device_id_type=MESH,
                    ))
                    sent[-1].start()
    for d in range(1, z.tp):
        source = lax.rem(s + d, z.tp)
        for m in range(3):
            landed = pin.at[source, m]
            pltpu.make_async_copy(landed, landed, p_recv.at[source * 3 + m]).wait()

    for t in range(z.tp):
        sums = []
        for m in range(3):
            value = pout[m, t]
            for d in range(1, z.tp):
                value += pin[lax.rem(s + d, z.tp), m, t]
            sums.append(value)
        gate, up, d_hidden = sums
        sig = jax.nn.sigmoid(gate)
        active = gate * sig
        hb[t, 0] = (d_hidden * up * sig * (1.0 + gate * (1.0 - sig))).astype(BF16)
        hb[t, 1] = (d_hidden * active).astype(BF16)
        hb[t, 2] = (active * up).astype(BF16)

    first = (((0,), (0,)), ((), ()))
    packed = jnp.zeros((z.hid, z.lanes), F32)
    for m in range(3):
        packed += lax.dot_general(hb[s, m], place[m], first, preferred_element_type=F32)
    lout[...] = packed.astype(BF16)
    for d in range(1, z.edp):
        sent.append(pltpu.make_async_remote_copy(
            src_ref=lout, dst_ref=lb.at[e], send_sem=l_send.at[d], recv_sem=l_recv.at[e],
            device_id=(i, lax.rem(e + d, z.edp), s), device_id_type=MESH,
        ))
        sent[-1].start()
    written = [pltpu.make_async_copy(lout, left.at[e], out_sem.at[0])]
    written[-1].start()

    owner = e // z.nblk
    mine = e - owner * z.nblk

    def relay(d):
        return pltpu.make_async_remote_copy(
            src_ref=rb, dst_ref=rb, send_sem=q_send.at[d], recv_sem=q_recv.at[0],
            device_id=(i, e, lax.rem(s + d, z.tp)), device_id_type=MESH,
        )

    @pl.when(s == owner)
    def _():
        for source in range(z.ep):
            rb[e, source] = xin[source, mine]
        others = rb.at[pl.ds(0, z.edp - 1)]
        pltpu.make_async_copy(others, others, r_recv.at[0]).wait()
        for d in range(1, z.tp):
            relay(d).start()

    for b in range(z.nblk):
        block = pl.ds(b * z.block, z.block)
        out = jnp.zeros((z.rows, z.block), F32)
        back = jnp.zeros((z.rows, z.block), F32)
        for t in range(z.tp):
            out += jnp.dot(hb[t, 2], wb[t, 2, :, block], preferred_element_type=F32)
            back += jnp.dot(hb[t, 0], wb[t, 0, :, block], preferred_element_type=F32)
            back += jnp.dot(hb[t, 1], wb[t, 1, :, block], preferred_element_type=F32)
        ob[:z.rows] = out.astype(BF16)
        ob[z.rows:] = back.astype(BF16)
        total = jnp.zeros((z.ep * z.xr, z.cw), F32)
        for q in range(z.nch):
            total += jnp.dot(perm_t[q], ob[:, q * z.cw:(q + 1) * z.cw], preferred_element_type=F32)
        y[:, b] = total.astype(BF16).reshape(z.ep, z.xr, z.cw)
        for d in range(1, z.ep):
            to = lax.rem(i + d, z.ep)
            sent.append(pltpu.make_async_remote_copy(
                src_ref=y.at[to, b], dst_ref=yin.at[i, b],
                send_sem=y_send.at[d * z.nblk + b], recv_sem=y_recv.at[i * z.nblk + b],
                device_id=(to, e, s), device_id_type=MESH,
            ))
            sent[-1].start()
    yin[i] = y[i]

    @pl.when(s != owner)
    def _():
        pltpu.make_async_copy(rb, rb, q_recv.at[0]).wait()

    for r in range(z.edp):
        flat = jnp.dot(
            factor[...], rb[r].reshape(z.ep * z.xr, z.cw), preferred_element_type=F32
        ).astype(BF16)
        for q in range(z.nch):
            right[pl.ds(r * z.lanes, z.lanes), pl.ds(q * z.cw, z.cw)] = flat[
                q * z.lanes:(q + 1) * z.lanes
            ]
    for k, (source, target) in enumerate(((homes, homes_out), (right, right_out))):
        written.append(pltpu.make_async_copy(source, target, out_sem.at[z.edp + k]))
        written[-1].start()

    for b in range(z.nblk):
        for d in range(1, z.ep):
            source = lax.rem(i + d, z.ep)
            landed = yin.at[source, b]
            pltpu.make_async_copy(landed, landed, y_recv.at[source * z.nblk + b]).wait()
        for w in range(z.window):
            total = yin[w * PARTS, b].astype(F32)
            for h in range(1, PARTS):
                total += yin[w * PARTS + h, b].astype(F32)
            summed[w, b] = (total * scales[w][1]).astype(BF16)
    written.append(pltpu.make_async_copy(summed, summed_out, out_sem.at[z.edp + 2]))
    written[-1].start()

    for d in range(1, z.edp):
        source = lax.rem(e + d, z.edp)
        landed = lb.at[source]
        pltpu.make_async_copy(landed, landed, l_recv.at[source]).wait()
        written.append(pltpu.make_async_copy(landed, left.at[source], out_sem.at[d]))
        written[-1].start()

    for copy in sent:
        copy.wait_send()
    for copy in written:
        copy.wait()
    for b in range(z.nblk):
        @pl.when(s * z.nblk + b != e)
        def _():
            for d in range(z.ep):
                right_copy(b, d).wait_send()

    @pl.when(s == owner)
    def _():
        for d in range(1, z.tp):
            relay(d).wait_send()


def finish(
    z, left_in, right_in, summed_in, homes_in, mixed, grad_tok, wgrad,
    left, right, summed, homes, wg, mix, grad, in_sem, sem,
):
    loads = [
        pltpu.make_async_copy(source, target, in_sem.at[k])
        for k, (source, target) in enumerate(
            ((summed_in, summed), (homes_in, homes), (left_in, left), (right_in, right))
        )
    ]
    for copy in loads:
        copy.start()
    lane = lax.broadcasted_iota(jnp.int32, (1, z.lanes), 1)
    width = z.ep * CAP
    keeps = [((lane >= m * width) & (lane < (m + 1) * width)).astype(F32).astype(BF16) for m in range(3)]
    loads[0].wait()
    loads[1].wait()
    copies = []
    for b in range(z.nblk):
        value = jnp.zeros((2 * z.nch * z.tok_rows, z.cw), F32)
        for w in range(z.window):
            home = homes[w].reshape(2 * z.nch * z.tok_rows, z.xr)
            value += jnp.dot(home, summed[w, b], preferred_element_type=F32)
        for q in range(z.nch):
            cols = pl.ds(b * z.block + q * z.cw, z.cw)
            for a, target in ((0, mix), (1, grad)):
                at = (2 * q + a) * z.tok_rows
                target[:, cols] = value[at:at + z.tok_rows].astype(BF16)
    for a, target in ((0, mix), (1, grad)):
        copies.append(pltpu.make_async_copy(target, (mixed, grad_tok)[a], sem.at[3 + a]))
        copies[-1].start()
    loads[2].wait()
    loads[3].wait()
    for m in range(3):
        factors = jnp.concatenate([left[r] * keeps[m] for r in range(z.edp)], axis=1)
        wg[m] = jnp.dot(factors, right[...], preferred_element_type=F32)
        copies.append(pltpu.make_async_copy(wg.at[m], wgrad.at[m], sem.at[m]))
        copies[-1].start()
    for copy in copies:
        copy.wait()


def shards(tokens, cotangent, expert_ids, route_weights, expert_weights):
    z = Sizes(
        lax.axis_size("ep"), lax.axis_size("edp"), lax.axis_size("tp"),
        tokens.shape[0], tokens.shape[1], expert_weights.shape[1],
    )
    tables = [jnp.asarray(table, BF16) for table in permutations(z)]
    operands = [tokens, cotangent, expert_ids.T, route_weights.T] + tables
    hbm = pl.BlockSpec(memory_space=pltpu.HBM)
    dma = pltpu.SemaphoreType.DMA
    between = (
        jax.ShapeDtypeStruct((z.edp, z.hid, z.lanes), BF16),
        jax.ShapeDtypeStruct((z.edp * z.lanes, z.block), BF16),
        jax.ShapeDtypeStruct((z.window, z.nblk, z.xr, z.cw), BF16),
        jax.ShapeDtypeStruct((z.window, 2 * z.nch, z.tok_rows, z.xr), BF16),
    )
    passed = pl.pallas_call(
        functools.partial(kernel, z),
        out_shape=between,
        in_specs=[hbm] * (len(operands) + 1),
        out_specs=(hbm,) * 4,
        scratch_shapes=[pltpu.VMEM(o.shape, o.dtype) for o in operands] + [
            pltpu.VMEM((z.tp, 3, z.hid, z.feats), BF16),
            pltpu.VMEM((z.window, z.nblk, z.xr, z.cw), BF16),
            pltpu.VMEM((z.ep, z.nblk, z.xr, z.cw), BF16),
            pltpu.VMEM((z.edp, z.ep, z.xr, z.cw), BF16),
            pltpu.VMEM((2 * z.rows, z.feats), BF16),
            pltpu.VMEM((3, z.tp, z.rows, z.hid), F32),
            pltpu.VMEM((z.tp, 3, z.tp, z.rows, z.hid), F32),
            pltpu.VMEM((z.tp, 3, z.rows, z.hid), BF16),
            pltpu.VMEM((z.hid, z.lanes), BF16),
            pltpu.VMEM((z.edp, z.hid, z.lanes), BF16),
            pltpu.VMEM((2 * z.rows, z.block), BF16),
            pltpu.VMEM((z.ep, z.nblk, z.xr, z.cw), BF16),
            pltpu.VMEM((z.ep, z.nblk, z.xr, z.cw), BF16),
        ] + [pltpu.VMEM(o.shape, o.dtype) for o in between[1:]] + [
            dma((z.edp + 3,)), dma((len(operands),)), dma, dma((z.tp * z.nblk,)), dma((z.tp * z.nblk,)),
            dma((z.ep * z.nblk,)), dma((z.ep * z.nblk,)),
            dma((z.nblk * z.ep,)), dma((1,)), dma((z.tp * 3,)), dma((z.tp * 3,)),
            dma((z.edp,)), dma((z.edp,)), dma((z.ep * z.nblk,)), dma((z.ep * z.nblk,)),
            dma((z.tp,)), dma((1,)),
        ],
        compiler_params=pltpu.CompilerParams(
            collective_id=0, has_side_effects=True, vmem_limit_bytes=VMEM_LIMIT
        ),
        name="expert_block",
    )(*operands, expert_weights)
    return pl.pallas_call(
        functools.partial(finish, z),
        out_shape=(
            jax.ShapeDtypeStruct(tokens.shape, BF16),
            jax.ShapeDtypeStruct(tokens.shape, BF16),
            jax.ShapeDtypeStruct((3, z.hid, z.block), F32),
        ),
        in_specs=[hbm] * 4,
        out_specs=(hbm,) * 3,
        scratch_shapes=[pltpu.VMEM(o.shape, o.dtype) for o in between] + [
            pltpu.VMEM((3, z.hid, z.block), F32),
            pltpu.VMEM(tokens.shape, BF16),
            pltpu.VMEM(tokens.shape, BF16),
            dma((4,)), dma((5,)),
        ],
        compiler_params=pltpu.CompilerParams(vmem_limit_bytes=VMEM_LIMIT),
        name="finish",
    )(*passed)


def solution(mesh):
    placed = (
        P(("ep", "edp"), "tp"),
        P(("ep", "edp"), "tp"),
        P(("ep", "edp"), None),
        P(("ep", "edp"), None),
        P(None, ("ep", "tp"), None),
    )
    return jax.shard_map(
        shards,
        mesh=mesh,
        in_specs=placed,
        out_specs=(P(("ep", "edp"), "tp"), P(("ep", "edp"), "tp"), P(None, ("ep", "tp"), "edp")),
        check_vma=False,
    )
```

profile of v0, /device:TPU:1, one launch (start us, length us, event | category | flops | bytes accessed | tf_op | source)
XLA Modules:
  0.0 27.9 jit_solution(12943573475736737920)
XLA Ops:
  0.6 24.0 %expert_block.1 = (bf16[4,192,128]{2,1,0:T(8,128)(2,1)}, bf16[512,1024]{1,0:T(8,128)(2,1)}, bf16[1,2,80,256]{3,2,1,0:T(8,128)(2,1)}, bf16[1,8,128,80]{3,2,1,0:T(8,128)(2,1)}) custom-call(bf16[128,2048]{1,0:T(8,128)(2,1)} %tok_in.1, bf16[128,2048]{1,0:T(8,128)(2,1)} %cot_in.1, s32[8,128]{1,0:T(8,128)} %bitcast.2, f32[8,128]{1,0:T(8,128)} %bitcast.3, ...), custom_call_target="tpu_custom_call" | custom-call | tf_op jit(solution)/shard_map/expert_block/pallas_call | solution.py:417
  24.6 3.3 %finish.1 = (bf16[128,2048]{1,0:T(8,128)(2,1)}, bf16[128,2048]{1,0:T(8,128)(2,1)}, f32[3,192,1024]{2,1,0:T(8,128)}) custom-call(bf16[4,192,128]{2,1,0:T(8,128)(2,1)} %get-tuple-element.7.left_in, bf16[512,1024]{1,0:T(8,128)(2,1)} %get-tuple-element.8.right_in, bf16[1,2,80,256]{3,2,1,0:T(8,128)(2,1)} %get-tuple-element.9.summed_in, ...), custom_call_target="tpu_custom_call" | custom-call | tf_op jit(solution)/shard_map/finish/pallas_call | solution.py:448
where the time goes:
time: 28.1 us; the launch traced here: 27.9 us
  Pallas kernels  27.3 us (97%)
  between operations  0.64 us (2%)
    pallas_call x1, Pallas kernels, shards(): pl.pallas_call(functools.partial(kernel, z), out_shape=between, in_specs=...  24 us
    pallas_call x1, Pallas kernels, shards(): pl.pallas_call(functools.partial(finish, z), out_shape=(jax.ShapeDtypeStr...  3.31 us

commit v1 on v0

v1 whole, which is shorter than its diff:
```python
import functools
import math

import jax
import jax.numpy as jnp
import numpy as np
from jax import lax
from jax.experimental import pallas as pl
from jax.experimental.pallas import tpu as pltpu
from jax.sharding import PartitionSpec as P

CAP = 10
PARTS = 4
SUB = 2
VMEM_LIMIT = 40 * 1024 * 1024
MESH = pl.DeviceIdType.MESH
F32 = jnp.float32
BF16 = jnp.bfloat16


def round_up(value, unit):
    return -(-value // unit) * unit


class Sizes:
    def __init__(self, ep, edp, tp, tok_rows, feats, hid):
        self.ep, self.edp, self.tp = ep, edp, tp
        self.window = ep // PARTS
        self.tok_rows, self.feats, self.hid = tok_rows, feats, hid
        self.block = feats * tp // edp
        self.nblk = feats // self.block
        self.sub = SUB if self.block % (SUB * 512) == 0 else 1
        self.piece = self.block // self.sub
        self.npc = feats // self.piece
        self.nch = max(1, min(4, self.piece // 128, max(2, self.piece // 256)))
        self.cw = self.piece // self.nch
        self.xr = round_up(2 * CAP * self.nch, 8)
        self.rows = round_up(ep * CAP, 16)
        self.lanes = round_up(3 * ep * CAP, 128)
        self.both = tp * hid
        side = math.isqrt(ep)
        side = side if side * side == ep else ep
        steps = [(a, b) for a in range(ep // side) for b in range(side) if a or b]
        self.side, self.steps = side, sorted(steps, key=lambda ab: -(bool(ab[0]) + bool(ab[1])))


def permutations(z):
    table = np.zeros((z.nch, 2, z.rows, z.ep, z.xr), np.float32)
    factor = np.zeros((z.nch, z.lanes, z.ep, z.xr), np.float32)
    place = np.zeros((3, z.rows, z.lanes), np.float32)
    for i in range(z.ep):
        for c in range(CAP):
            for q in range(z.nch):
                for a in range(2):
                    table[q, a, i * CAP + c, i, (2 * q + a) * CAP + c] = 1.0
                for m in range(3):
                    factor[q, (m * z.ep + i) * CAP + c, i, (2 * q + m // 2) * CAP + c] = 1.0
            for m in range(3):
                place[m, i * CAP + c, (m * z.ep + i) * CAP + c] = 1.0
    flat = table.reshape(z.nch * 2 * z.rows, z.ep * z.xr)
    return flat, flat.T.copy(), factor.reshape(-1, z.ep * z.xr), place


def slot_parts(index, nch):
    chunk = jnp.zeros_like(index)
    for k in range(1, nch):
        chunk += (index >= 2 * CAP * k).astype(jnp.int32)
    rest = index - 2 * CAP * chunk
    array = (rest >= CAP).astype(jnp.int32)
    return chunk, array, rest - CAP * array


def landed(ref, sem):
    pltpu.make_async_copy(ref, ref, sem).wait()


def kernel(
    z, tok_in, cot_in, ids_in, rw_in, perm_in, perm_t_in, factor_in, place_in, weights,
    wg, summed, homes,
    tok, cot, ids, rw, perm, perm_t, factor, place,
    wb, x, xin, zb, rb, rows, pout, pin, hgu, hh, hs, lb, ob, y, yin, right,
    in_sem, w_loc, w_send, w_recv, x_send, x_recv, z_send, z_recv, r_send, r_recv, p_send, p_recv,
    l_send, l_recv, y_send, y_recv, q_send, q_recv, upper,
):
    i, e, s = lax.axis_index("ep"), lax.axis_index("edp"), lax.axis_index("tp")
    barrier = pltpu.get_barrier_semaphore()
    down, across = i // z.side, lax.rem(i, z.side)
    peers = [
        lax.rem(down + a, z.ep // z.side) * z.side + lax.rem(across + b, z.side) for a, b in z.steps
    ]

    loads = [
        pltpu.make_async_copy(source, target, in_sem.at[k])
        for k, (source, target) in enumerate((
            (ids_in, ids), (rw_in, rw), (tok_in, tok), (cot_in, cot),
            (perm_in, perm), (perm_t_in, perm_t), (factor_in, factor), (place_in, place),
        ))
    ]
    for copy in loads[:4]:
        copy.start()

    for to in peers:
        pl.semaphore_signal(barrier, inc=1, device_id=(to, e, s), device_id_type=MESH)
    for d in range(1, z.tp):
        pl.semaphore_signal(barrier, inc=1, device_id=(i, e, lax.rem(s + d, z.tp)), device_id_type=MESH)
    for d in range(1, z.edp):
        @pl.when(e + d < z.edp)
        def _():
            pl.semaphore_signal(barrier, inc=1, device_id=(i, e + d, s), device_id_type=MESH)

    own_w = pltpu.make_async_copy(
        weights.at[:, :, pl.ds(pl.multiple_of(s * z.feats, 128), z.feats)], wb.at[:, s], w_loc
    )
    own_w.start()
    for copy in loads[4:]:
        copy.start()

    row = lax.broadcasted_iota(jnp.int32, (z.xr, z.tok_rows), 0)
    chunk, array, slot = slot_parts(row, z.nch)
    in_use = row < 2 * CAP * z.nch
    before = (
        lax.broadcasted_iota(jnp.int32, (z.tok_rows, z.tok_rows), 0)
        < lax.broadcasted_iota(jnp.int32, (z.tok_rows, z.tok_rows), 1)
    ).astype(F32).astype(BF16)
    lane = lax.broadcasted_iota(jnp.int32, (z.tok_rows, z.xr), 1)
    lane_chunk, lane_array, _ = slot_parts(lane, z.nch)
    loads[0].wait()
    loads[1].wait()
    ids_t = ids[...]
    rw_t = rw[...]
    chosen, scales, picks = [], [], []
    for w in range(z.window):
        hit = (ids_t == w).astype(F32)
        match = jnp.sum(hit, axis=0, keepdims=True)
        weight = jnp.sum(hit * rw_t, axis=0, keepdims=True)
        match_all = jnp.broadcast_to(match, (z.xr, z.tok_rows))
        rank = jnp.dot(match_all.astype(BF16), before, preferred_element_type=F32)
        pick = jnp.where(in_use & (rank == slot.astype(F32)), match_all, 0.0)
        slot_weight = jnp.sum(pick * weight, axis=1, keepdims=True)
        picks.append(pick)
        scales.append((
            jnp.where(array[:, :1] == 1, slot_weight, 1.0), jnp.where(array[:, :1] == 0, slot_weight, 1.0),
        ))
        chosen.append([
            [jnp.where((chunk == q) & (array == a), pick, 0.0).astype(BF16) for a in range(2)]
            for q in range(z.nch)
        ])
    loads[2].wait()
    loads[3].wait()

    def gather(p):
        for w in range(z.window):
            total = jnp.zeros((z.xr, z.cw), F32)
            for q in range(z.nch):
                cols = pl.ds(p * z.piece + q * z.cw, z.cw)
                for a, source in ((0, tok), (1, cot)):
                    total += jnp.dot(chosen[w][q][a], source[:, cols], preferred_element_type=F32)
            x[w, p] = (total * scales[w][0]).astype(BF16)

    sent = []

    def send(source, target, send_sem, recv_sem, to):
        sent.append(pltpu.make_async_remote_copy(
            src_ref=source, dst_ref=target, send_sem=send_sem, recv_sem=recv_sem,
            device_id=to, device_id_type=MESH,
        ))
        sent[-1].start()

    for p in range(z.npc):
        gather(p)
        if p == 0:
            pl.semaphore_wait(barrier, z.ep - 1 + z.tp - 1 + e)
        for k, to in enumerate(peers):
            send(
                x.at[to // PARTS, p], xin.at[i, p],
                x_send.at[k * z.npc + p], x_recv.at[i * z.npc + p], (to, e, s),
            )
        if p == 0:
            for b in range(z.nblk):
                for d in range(1, z.tp):
                    to = lax.rem(s + d, z.tp)
                    cols = pl.ds(pl.multiple_of(to * z.feats + b * z.block, 128), z.block)
                    send(
                        weights.at[:, :, cols], wb.at[:, s, :, pl.ds(b * z.block, z.block)],
                        w_send.at[d * z.nblk + b], w_recv.at[s * z.nblk + b], (i, e, to),
                    )
    for d in range(1, z.edp):
        @pl.when(e - d >= 0)
        def _():
            pl.semaphore_signal(upper, inc=1, device_id=(i, e - d, s), device_id_type=MESH)

    for p in range(z.npc):
        xin[i, p] = x[i // PARTS, p]
    for w in range(z.window):
        home = jnp.transpose(picks[w])
        for q in range(z.nch):
            for a in range(2):
                homes[w, 2 * q + a] = jnp.where(
                    (lane_chunk == q) & (lane_array == a), home, 0.0
                ).astype(BF16)

    def replica_copy(b):
        to = s * z.nblk + b
        slot_at = lax.rem(e - to + z.edp, z.edp) - 1
        return pltpu.make_async_remote_copy(
            src_ref=x.at[:, pl.ds(b * z.sub, z.sub)], dst_ref=zb.at[slot_at],
            send_sem=z_send.at[b], recv_sem=z_recv.at[slot_at],
            device_id=(i, to, s), device_id_type=MESH,
        )

    @pl.when(e < z.edp - 1)
    def _():
        pl.semaphore_wait(upper, z.edp - 1 - e)

    for b in range(z.nblk):
        @pl.when(s * z.nblk + b != e)
        def _():
            replica_copy(b).start()

    own_w.wait()
    for copy in loads[4:]:
        copy.wait()

    owner = e // z.nblk
    mine = e - owner * z.nblk
    last = (((1,), (1,)), ((), ()))
    gu, dh = pl.ds(0, 2 * z.both), pl.ds(2 * z.both, z.both)
    for p in range(z.npc):
        for to in peers:
            landed(xin.at[to, p], x_recv.at[to * z.npc + p])
        flat = jnp.dot(
            perm[...], xin[:, p].reshape(z.ep * z.xr, z.cw), preferred_element_type=F32
        ).astype(BF16)
        for q in range(z.nch):
            rows[:, q * z.cw:(q + 1) * z.cw] = flat[q * 2 * z.rows:(q + 1) * 2 * z.rows]
        if p % z.sub == 0:
            b = p // z.sub
            for d in range(1, z.tp):
                source = lax.rem(s + d, z.tp)
                landed(wb.at[:, source, :, pl.ds(b * z.block, z.block)], w_recv.at[source * z.nblk + b])
        cols = pl.ds(p * z.piece, z.piece)
        for part, which, at in ((rows[:z.rows], pl.ds(0, 2), gu), (rows[z.rows:], pl.ds(2, 1), dh)):
            value = lax.dot_general(
                part, wb[which, :, :, cols].reshape(-1, z.piece), last, preferred_element_type=F32
            )
            if p:
                value += pout[:, at]
            pout[:, at] = value
            if p == z.npc - 1:
                for d in range(1, z.tp):
                    k = 0 if at is gu else 1
                    send(
                        pout.at[:, at], pin.at[s, :, at],
                        p_send.at[d * 2 + k], p_recv.at[s * 2 + k], (i, e, lax.rem(s + d, z.tp)),
                    )

    def spread_copy(k, to):
        return pltpu.make_async_remote_copy(
            src_ref=zb.at[:, to // PARTS], dst_ref=rb.at[pl.ds(1, z.edp - 1), i],
            send_sem=r_send.at[k], recv_sem=r_recv.at[i],
            device_id=(to, e, s), device_id_type=MESH,
        )

    @pl.when(s == owner)
    def _():
        for d in range(1, z.edp):
            landed(zb.at[d - 1], z_recv.at[d - 1])
        for k, to in enumerate(peers):
            spread_copy(k, to).start()

    for d in range(1, z.tp):
        source = lax.rem(s + d, z.tp)
        for k, at in enumerate((gu, dh)):
            landed(pin.at[source, :, at], p_recv.at[source * 2 + k])

    sums = pout[...]
    for d in range(1, z.tp):
        sums += pin[lax.rem(s + d, z.tp)]
    gate, up, d_hidden = (sums[:, m * z.both:(m + 1) * z.both] for m in range(3))
    sig = jax.nn.sigmoid(gate)
    active = gate * sig
    hh[...] = (active * up).astype(BF16)
    hgu[:, :z.both] = (d_hidden * up * sig * (1.0 + gate * (1.0 - sig))).astype(BF16)
    hgu[:, z.both:] = (d_hidden * active).astype(BF16)

    def output(p):
        cols = pl.ds(p * z.piece, z.piece)
        out = jnp.dot(hh[...], wb[2, :, :, cols].reshape(-1, z.piece), preferred_element_type=F32)
        back = jnp.dot(hgu[...], wb[:2, :, :, cols].reshape(-1, z.piece), preferred_element_type=F32)
        for q in range(z.nch):
            for a, value in enumerate((out, back)):
                at = (2 * q + a) * z.rows
                ob[at:at + z.rows] = value[:, q * z.cw:(q + 1) * z.cw].astype(BF16)
        total = jnp.dot(perm_t[...], ob[...], preferred_element_type=F32)
        y[:, p] = total.astype(BF16).reshape(z.ep, z.xr, z.cw)
        for k, to in enumerate(peers):
            send(
                y.at[to, p], yin.at[i, p],
                y_send.at[k * z.npc + p], y_recv.at[i * z.npc + p], (to, e, s),
            )

    first = (((0,), (0,)), ((), ()))
    output(0)
    for t in range(z.tp):
        at = slice(t * z.hid, (t + 1) * z.hid)
        hs[t, 0] = hgu[:, at]
        hs[t, 1] = hgu[:, z.both + t * z.hid:z.both + (t + 1) * z.hid]
        hs[t, 2] = hh[:, at]
    packed = jnp.zeros((z.hid, z.lanes), F32)
    for m in range(3):
        packed += lax.dot_general(hs[s, m], place[m], first, preferred_element_type=F32)
    lb[0] = packed.astype(BF16)
    upward = (2 * e) // z.edp
    for k in range(z.edp - 1):
        low = k + (k - e + z.edp) // z.edp
        high = z.edp - 1 - k
        high = high - (e - high + z.edp) // z.edp
        to = upward * low + (1 - upward) * high
        slot_at = lax.rem(e - to + z.edp, z.edp)
        send(lb.at[0], lb.at[slot_at], l_send.at[k], l_recv.at[slot_at], (i, to, s))
    for p in range(1, z.npc):
        output(p)
    yin[i] = y[i]

    def relay(d):
        return pltpu.make_async_remote_copy(
            src_ref=rb, dst_ref=rb, send_sem=q_send.at[d], recv_sem=q_recv.at[0],
            device_id=(i, e, lax.rem(s + d, z.tp)), device_id_type=MESH,
        )

    @pl.when(s == owner)
    def _():
        for p in range(z.sub):
            rb[0, :, p] = xin[:, mine * z.sub + p]
        rb[1:, i] = zb[:, i // PARTS]
        for to in peers:
            landed(rb.at[pl.ds(1, z.edp - 1), to], r_recv.at[to])
        for d in range(1, z.tp):
            relay(d).start()

    @pl.when(s != owner)
    def _():
        landed(rb, q_recv.at[0])

    for r in range(z.edp):
        for p in range(z.sub):
            flat = jnp.dot(
                factor[...], rb[r, :, p].reshape(z.ep * z.xr, z.cw), preferred_element_type=F32
            ).astype(BF16)
            for q in range(z.nch):
                right[pl.ds(r * z.lanes, z.lanes), pl.ds(p * z.piece + q * z.cw, z.cw)] = flat[
                    q * z.lanes:(q + 1) * z.lanes
                ]

    for p in range(z.npc):
        for to in peers:
            landed(yin.at[to, p], y_recv.at[to * z.npc + p])
        for w in range(z.window):
            total = yin[w * PARTS, p].astype(F32)
            for h in range(1, PARTS):
                total += yin[w * PARTS + h, p].astype(F32)
            summed[w, p] = (total * scales[w][1]).astype(BF16)

    for d in range(1, z.edp):
        landed(lb.at[d], l_recv.at[d])
    lane = lax.broadcasted_iota(jnp.int32, (1, z.lanes), 1)
    width = z.ep * CAP
    for m in range(3):
        keep = ((lane >= m * width) & (lane < (m + 1) * width)).astype(F32).astype(BF16)
        factors = jnp.concatenate([lb[r] * keep for r in range(z.edp)], axis=1)
        wg[m] = jnp.dot(factors, right[...], preferred_element_type=F32)

    for copy in sent:
        copy.wait_send()
    for b in range(z.nblk):
        @pl.when(s * z.nblk + b != e)
        def _():
            replica_copy(b).wait_send()

    @pl.when(s == owner)
    def _():
        for k, to in enumerate(peers):
            spread_copy(k, to).wait_send()
        for d in range(1, z.tp):
            relay(d).wait_send()


def finish(z, wg, summed, homes, mixed, grad_tok, wgrad, mix, grad, sem):
    copies = []
    for m in range(3):
        copies.append(pltpu.make_async_copy(wg.at[m], wgrad.at[m], sem.at[m]))
        copies[-1].start()
    for p in range(z.npc):
        value = jnp.zeros((2 * z.nch * z.tok_rows, z.cw), F32)
        for w in range(z.window):
            home = homes[w].reshape(2 * z.nch * z.tok_rows, z.xr)
            value += jnp.dot(home, summed[w, p], preferred_element_type=F32)
        for q in range(z.nch):
            cols = pl.ds(p * z.piece + q * z.cw, z.cw)
            for a, target in ((0, mix), (1, grad)):
                at = (2 * q + a) * z.tok_rows
                target[:, cols] = value[at:at + z.tok_rows].astype(BF16)
    for a, target in ((0, mix), (1, grad)):
        copies.append(pltpu.make_async_copy(target, (mixed, grad_tok)[a], sem.at[3 + a]))
        copies[-1].start()
    for copy in copies:
        copy.wait()


def shards(tokens, cotangent, expert_ids, route_weights, expert_weights):
    z = Sizes(
        lax.axis_size("ep"), lax.axis_size("edp"), lax.axis_size("tp"),
        tokens.shape[0], tokens.shape[1], expert_weights.shape[1],
    )
    tables = [jnp.asarray(table, BF16) for table in permutations(z)]
    operands = [tokens, cotangent, expert_ids.T, route_weights.T] + tables
    hbm = pl.BlockSpec(memory_space=pltpu.HBM)
    vmem = pl.BlockSpec(memory_space=pltpu.VMEM)
    dma = pltpu.SemaphoreType.DMA
    passed = pl.pallas_call(
        functools.partial(kernel, z),
        out_shape=(
            pltpu.VMEM((3, z.hid, z.block), F32),
            pltpu.VMEM((z.window, z.npc, z.xr, z.cw), BF16),
            pltpu.VMEM((z.window, 2 * z.nch, z.tok_rows, z.xr), BF16),
        ),
        in_specs=[hbm] * (len(operands) + 1),
        out_specs=(vmem,) * 3,
        scratch_shapes=[pltpu.VMEM(o.shape, o.dtype) for o in operands] + [
            pltpu.VMEM((3, z.tp, z.hid, z.feats), BF16),
            pltpu.VMEM((z.window, z.npc, z.xr, z.cw), BF16),
            pltpu.VMEM((z.ep, z.npc, z.xr, z.cw), BF16),
            pltpu.VMEM((z.edp - 1, z.window, z.sub, z.xr, z.cw), BF16),
            pltpu.VMEM((z.edp, z.ep, z.sub, z.xr, z.cw), BF16),
            pltpu.VMEM((2 * z.rows, z.piece), BF16),
            pltpu.VMEM((z.rows, 3 * z.both), F32),
            pltpu.VMEM((z.tp, z.rows, 3 * z.both), F32),
            pltpu.VMEM((z.rows, 2 * z.both), BF16),
            pltpu.VMEM((z.rows, z.both), BF16),
            pltpu.VMEM((z.tp, 3, z.rows, z.hid), BF16),
            pltpu.VMEM((z.edp, z.hid, z.lanes), BF16),
            pltpu.VMEM((z.nch * 2 * z.rows, z.cw), BF16),
            pltpu.VMEM((z.ep, z.npc, z.xr, z.cw), BF16),
            pltpu.VMEM((z.ep, z.npc, z.xr, z.cw), BF16),
            pltpu.VMEM((z.edp * z.lanes, z.block), BF16),
        ] + [
            dma((len(operands),)), dma, dma((z.tp * z.nblk,)), dma((z.tp * z.nblk,)),
            dma((z.ep * z.npc,)), dma((z.ep * z.npc,)),
            dma((z.nblk,)), dma((z.edp - 1,)), dma((z.ep,)), dma((z.ep,)),
            dma((z.tp * 2,)), dma((z.tp * 2,)),
            dma((z.edp,)), dma((z.edp,)), dma((z.ep * z.npc,)), dma((z.ep * z.npc,)),
            dma((z.tp,)), dma((1,)), pltpu.SemaphoreType.REGULAR,
        ],
        compiler_params=pltpu.CompilerParams(
            collective_id=0, has_side_effects=True, vmem_limit_bytes=VMEM_LIMIT
        ),
        name="expert_block",
    )(*[pltpu.with_memory_space_constraint(o, pltpu.HBM) for o in (*operands, expert_weights)])
    return pl.pallas_call(
        functools.partial(finish, z),
        out_shape=(
            jax.ShapeDtypeStruct(tokens.shape, BF16),
            jax.ShapeDtypeStruct(tokens.shape, BF16),
            jax.ShapeDtypeStruct((3, z.hid, z.block), F32),
        ),
        in_specs=[vmem] * 3,
        out_specs=(hbm,) * 3,
        scratch_shapes=[
            pltpu.VMEM(tokens.shape, BF16),
            pltpu.VMEM(tokens.shape, BF16),
            dma((5,)),
        ],
        compiler_params=pltpu.CompilerParams(vmem_limit_bytes=VMEM_LIMIT),
        name="finish",
    )(*[pltpu.with_memory_space_constraint(o, pltpu.VMEM) for o in passed])


def solution(mesh):
    placed = (
        P(("ep", "edp"), "tp"),
        P(("ep", "edp"), "tp"),
        P(("ep", "edp"), None),
        P(("ep", "edp"), None),
        P(None, ("ep", "tp"), None),
    )
    return jax.shard_map(
        shards,
        mesh=mesh,
        in_specs=placed,
        out_specs=(P(("ep", "edp"), "tp"), P(("ep", "edp"), "tp"), P(None, ("ep", "tp"), "edp")),
        check_vma=False,
    )
```

time: 28.1 us -> 24.6 us (0.88); the launches traced: 27.9 us -> 24.1 us
  Pallas kernels: 27.3 us -> 23.5 us
    pallas_call x1, Pallas kernels: 24 us -> 21.7 us  [shards(): pl.pallas_call(functools.partial(kernel, z), out_shape=(pltpu.VMEM((3, z....]
    pallas_call x1, Pallas kernels: 3.31 us -> 1.79 us  [shards(): pl.pallas_call(functools.partial(finish, z), out_shape=(jax.ShapeDtypeStr...]
where the time goes in v1:
time: 24.6 us; the launch traced here: 24.1 us
  Pallas kernels  23.5 us (96%)
  between operations  0.64 us (3%)
    pallas_call x1, Pallas kernels, shards(): pl.pallas_call(functools.partial(kernel, z), out_shape=(pltpu.VMEM((3, z....  21.7 us
    pallas_call x1, Pallas kernels, shards(): pl.pallas_call(functools.partial(finish, z), out_shape=(jax.ShapeDtypeStr...  1.79 us

profile of v1, /device:TPU:1, one launch (start us, length us, event | category | flops | bytes accessed | tf_op | source)
XLA Modules:
  0.0 24.1 jit_solution(8308978327599519971)
XLA Ops:
  0.6 21.7 %expert_block.1 = (f32[3,192,1024]{2,1,0:T(8,128)S(1)}, bf16[1,4,40,256]{3,2,1,0:T(8,128)(2,1)S(1)}, bf16[1,4,128,40]{3,2,1,0:T(8,128)(2,1)S(1)}) custom-call(bf16[128,2048]{1,0:T(8,128)(2,1)} %tok_in.1, bf16[128,2048]{1,0:T(8,128)(2,1)} %cot_in.1, s32[8,128]{1,0:T(8,128)} %bitcast.2, f32[8,128]{1,0:T(8,128)} %bitcast.3, ...), custom_call_target="tpu_custom_call" | custom-call | tf_op jit(solution)/shard_map/expert_block/pallas_call | solution.py:420
  22.4 1.8 %finish.1 = (bf16[128,2048]{1,0:T(8,128)(2,1)}, bf16[128,2048]{1,0:T(8,128)(2,1)}, f32[3,192,1024]{2,1,0:T(8,128)}) custom-call(f32[3,192,1024]{2,1,0:T(8,128)S(1)} %get-tuple-element.6.wg, bf16[1,4,40,256]{3,2,1,0:T(8,128)(2,1)S(1)} %get-tuple-element.7.summed, bf16[1,4,128,40]{3,2,1,0:T(8,128)(2,1)S(1)} %get-tuple-element.8.homes), custom_call_target="tpu_custom_call" | custom-call | tf_op jit(solution)/shard_map/finish/pallas_call | solution.py:459

commit v2 on v1

v2 whole, which is shorter than its diff:
```python
import functools
import math

import jax
import jax.numpy as jnp
import numpy as np
from jax import lax
from jax.experimental import pallas as pl
from jax.experimental.pallas import tpu as pltpu
from jax.sharding import PartitionSpec as P

CAP = 10
PARTS = 4
SUB = 2
VMEM_LIMIT = 40 * 1024 * 1024
MESH = pl.DeviceIdType.MESH
F32 = jnp.float32
BF16 = jnp.bfloat16


def round_up(value, unit):
    return -(-value // unit) * unit


class Sizes:
    def __init__(self, ep, edp, tp, tok_rows, feats, hid):
        self.ep, self.edp, self.tp = ep, edp, tp
        self.window = ep // PARTS
        self.tok_rows, self.feats, self.hid = tok_rows, feats, hid
        self.block = feats * tp // edp
        self.nblk = feats // self.block
        self.sub = SUB if self.block % (SUB * 512) == 0 else 1
        self.piece = self.block // self.sub
        self.npc = feats // self.piece
        self.nch = max(1, min(4, self.piece // 128, max(2, self.piece // 256)))
        self.cw = self.piece // self.nch
        self.xr = round_up(2 * CAP * self.nch, 8)
        self.rows = round_up(ep * CAP, 16)
        self.lanes = round_up(3 * ep * CAP, 128)
        self.both = tp * hid
        wide, tall = ep * self.xr, self.nch * 2 * self.rows
        self.tables, at = [], 0
        for n, width in ((tall, wide), (wide, tall), (self.nch * self.lanes, wide), (3 * self.rows, self.lanes)):
            self.tables.append((at, n, width))
            at += n
        self.table_lanes = round_up(max(width for _, _, width in self.tables), 128)
        side = math.isqrt(ep)
        side = side if side * side == ep else ep
        steps = [(a, b) for a in range(ep // side) for b in range(side) if a or b]
        self.side, self.steps = side, sorted(steps, key=lambda ab: -(bool(ab[0]) + bool(ab[1])))


def permutations(z):
    table = np.zeros((z.nch, 2, z.rows, z.ep, z.xr), np.float32)
    factor = np.zeros((z.nch, z.lanes, z.ep, z.xr), np.float32)
    place = np.zeros((3, z.rows, z.lanes), np.float32)
    for i in range(z.ep):
        for c in range(CAP):
            for q in range(z.nch):
                for a in range(2):
                    table[q, a, i * CAP + c, i, (2 * q + a) * CAP + c] = 1.0
                for m in range(3):
                    factor[q, (m * z.ep + i) * CAP + c, i, (2 * q + m // 2) * CAP + c] = 1.0
            for m in range(3):
                place[m, i * CAP + c, (m * z.ep + i) * CAP + c] = 1.0
    flat = table.reshape(z.nch * 2 * z.rows, z.ep * z.xr)
    packed = np.zeros((sum(n for _, n, _ in z.tables), z.table_lanes), np.float32)
    for (at, n, width), part in zip(z.tables, (flat, flat.T, factor, place), strict=True):
        packed[at:at + n, :width] = part.reshape(n, width)
    return packed


def slot_parts(index, nch):
    chunk = jnp.zeros_like(index)
    for k in range(1, nch):
        chunk += (index >= 2 * CAP * k).astype(jnp.int32)
    rest = index - 2 * CAP * chunk
    array = (rest >= CAP).astype(jnp.int32)
    return chunk, array, rest - CAP * array


def landed(ref, sem):
    pltpu.make_async_copy(ref, ref, sem).wait()


def kernel(
    z, tok_in, cot_in, ids_in, rw_in, tables_in, weights,
    wg, summed, homes,
    data, ids, rw, tables,
    wb, x, xin, zb, rb, rows, pout, pin, hgu, hh, hs, lb, ob, y, yin, right,
    in_sem, w_loc, w_send, w_recv, x_send, x_recv, z_send, z_recv, r_send, r_recv, p_send, p_recv,
    l_send, l_recv, y_send, y_recv, q_send, q_recv, ep_ready, edp_ready, tp_ready,
):
    i, e, s = lax.axis_index("ep"), lax.axis_index("edp"), lax.axis_index("tp")
    barrier = pltpu.get_barrier_semaphore()
    down, across = i // z.side, lax.rem(i, z.side)
    peers = [
        lax.rem(down + a, z.ep // z.side) * z.side + lax.rem(across + b, z.side) for a, b in z.steps
    ]
    partners = [lax.rem(s + d, z.tp) for d in range(1, z.tp)]
    perm, perm_t, factor, place = (tables.at[pl.ds(at, n), pl.ds(0, width)] for at, n, width in z.tables)

    loads = [
        pltpu.make_async_copy(ids_in, ids, in_sem.at[0]),
        pltpu.make_async_copy(rw_in, rw, in_sem.at[1]),
        pltpu.make_async_copy(tok_in, data.at[0], in_sem.at[2]),
        pltpu.make_async_copy(cot_in, data.at[1], in_sem.at[2]),
    ]
    for copy in loads:
        copy.start()

    def signal(semaphore, condition, to):
        @pl.when(condition)
        def _():
            pl.semaphore_signal(semaphore, inc=1, device_id=to, device_id_type=MESH)

    for to in partners:
        signal(barrier, to > s, (i, e, to))
    for to in peers:
        signal(barrier, to > i, (to, e, s))
    for d in range(1, z.edp):
        signal(barrier, e + d < z.edp, (i, lax.rem(e + d, z.edp), s))

    @pl.when(i + e + s > 0)
    def _():
        pl.semaphore_wait(barrier, i + e + s)

    for to in partners:
        signal(tp_ready, to < s, (i, e, to))
    for to in peers:
        signal(ep_ready.at[i], to < i, (to, e, s))
    for d in range(1, z.edp):
        signal(edp_ready, e - d >= 0, (i, lax.rem(e - d + z.edp, z.edp), s))

    @pl.when(s < z.tp - 1)
    def _():
        pl.semaphore_wait(tp_ready, z.tp - 1 - s)

    def send(source, target, send_sem, recv_sem, to):
        pltpu.make_async_remote_copy(
            src_ref=source, dst_ref=target, send_sem=send_sem, recv_sem=recv_sem,
            device_id=to, device_id_type=MESH,
        ).start()

    for b in range(z.nblk):
        for to in partners:
            cols = pl.ds(pl.multiple_of(to * z.feats + b * z.block, 128), z.block)
            send(
                weights.at[:, :, cols], wb.at[:, s, :, pl.ds(b * z.block, z.block)],
                w_send, w_recv.at[b], (i, e, to),
            )

    row = lax.broadcasted_iota(jnp.int32, (z.xr, z.tok_rows), 0)
    chunk, array, slot = slot_parts(row, z.nch)
    in_use = row < 2 * CAP * z.nch
    before = (
        lax.broadcasted_iota(jnp.int32, (z.tok_rows, z.tok_rows), 0)
        < lax.broadcasted_iota(jnp.int32, (z.tok_rows, z.tok_rows), 1)
    ).astype(F32).astype(BF16)
    lane = lax.broadcasted_iota(jnp.int32, (z.tok_rows, z.xr), 1)
    lane_chunk, lane_array, _ = slot_parts(lane, z.nch)
    loads[0].wait()
    loads[1].wait()
    ids_t = ids[...]
    rw_t = rw[...]
    chosen, scales, picks = [], [], []
    for w in range(z.window):
        hit = (ids_t == w).astype(F32)
        match = jnp.sum(hit, axis=0, keepdims=True)
        weight = jnp.sum(hit * rw_t, axis=0, keepdims=True)
        match_all = jnp.broadcast_to(match, (z.xr, z.tok_rows))
        rank = jnp.dot(match_all.astype(BF16), before, preferred_element_type=F32)
        pick = jnp.where(in_use & (rank == slot.astype(F32)), match_all, 0.0)
        slot_weight = jnp.sum(pick * weight, axis=1, keepdims=True)
        picks.append(pick)
        scales.append((
            jnp.where(array[:, :1] == 1, slot_weight, 1.0), jnp.where(array[:, :1] == 0, slot_weight, 1.0),
        ))
        chosen.append([
            [jnp.where((chunk == q) & (array == a), pick, 0.0).astype(BF16) for a in range(2)]
            for q in range(z.nch)
        ])
    landed(data, in_sem.at[2])
    own_w = pltpu.make_async_copy(
        weights.at[:, :, pl.ds(pl.multiple_of(s * z.feats, 128), z.feats)], wb.at[:, s], w_loc
    )
    own_w.start()
    table_load = pltpu.make_async_copy(tables_in, tables, in_sem.at[3])
    table_load.start()

    def send_rows(p, to):
        send(x.at[to // PARTS, p], xin.at[i, p], x_send, x_recv.at[p], (to, e, s))

    def send_replica(b):
        to = s * z.nblk + b
        slot_at = lax.rem(e - to + z.edp, z.edp) - 1
        send(x.at[:, pl.ds(b * z.sub, z.sub)], zb.at[slot_at], z_send, z_recv, (i, to, s))

    for p in range(z.npc):
        for w in range(z.window):
            total = jnp.zeros((z.xr, z.cw), F32)
            for q in range(z.nch):
                cols = pl.ds(p * z.piece + q * z.cw, z.cw)
                for a in range(2):
                    total += jnp.dot(chosen[w][q][a], data[a, :, cols], preferred_element_type=F32)
            x[w, p] = (total * scales[w][0]).astype(BF16)
        for to in peers:
            @pl.when(to < i)
            def _():
                send_rows(p, to)
    for to in reversed(peers):
        @pl.when(to > i)
        def _():
            pl.semaphore_wait(ep_ready.at[to], 1)
            for p in range(z.npc):
                send_rows(p, to)
    for b in range(z.nblk):
        @pl.when(s * z.nblk + b < e)
        def _():
            send_replica(b)

    for p in range(z.npc):
        xin[i, p] = x[i // PARTS, p]
    for w in range(z.window):
        home = jnp.transpose(picks[w])
        for q in range(z.nch):
            for a in range(2):
                homes[w, 2 * q + a] = jnp.where(
                    (lane_chunk == q) & (lane_array == a), home, 0.0
                ).astype(BF16)
    own_w.wait()
    table_load.wait()

    owner = e // z.nblk
    mine = e - owner * z.nblk
    last = (((1,), (1,)), ((), ()))
    for p in range(z.npc):
        landed(xin.at[pl.ds(0, z.ep - 1), p], x_recv.at[p])
        if p == 0:
            @pl.when(e < z.edp - 1)
            def _():
                pl.semaphore_wait(edp_ready, z.edp - 1 - e)

            for b in range(z.nblk):
                @pl.when(s * z.nblk + b > e)
                def _():
                    send_replica(b)
        flat = jnp.dot(
            perm[...], xin[:, p].reshape(z.ep * z.xr, z.cw), preferred_element_type=F32
        ).astype(BF16)
        for q in range(z.nch):
            rows[:, q * z.cw:(q + 1) * z.cw] = flat[q * 2 * z.rows:(q + 1) * 2 * z.rows]
        if p % z.sub == 0:
            b = p // z.sub
            landed(wb.at[:, pl.ds(0, z.tp - 1), :, pl.ds(b * z.block, z.block)], w_recv.at[b])
        cols = pl.ds(p * z.piece, z.piece)
        first_two = lax.dot_general(
            rows[:z.rows], wb[:2, :, :, cols].reshape(-1, z.piece), last, preferred_element_type=F32
        )
        third = lax.dot_general(
            rows[z.rows:], wb[2, :, :, cols].reshape(-1, z.piece), last, preferred_element_type=F32
        )
        if p:
            first_two += pout[:, :2 * z.both]
            third += pout[:, 2 * z.both:]
        pout[:, :2 * z.both] = first_two
        pout[:, 2 * z.both:] = third
    for to in partners:
        send(pout, pin.at[s], p_send, p_recv, (i, e, to))

    others = pl.ds(1, z.edp - 1)

    @pl.when(s == owner)
    def _():
        landed(zb, z_recv)
        for to in peers:
            send(zb.at[:, to // PARTS], rb.at[others, i], r_send, r_recv.at[i], (to, e, s))
        for k, to in enumerate(partners):
            send(
                xin.at[:, pl.ds(mine * z.sub, z.sub)], rb.at[0], q_send.at[k], q_recv, (i, e, to),
            )
            send(zb.at[:, i // PARTS], rb.at[others, i], q_send.at[k], q_recv, (i, e, to))

    landed(pin.at[pl.ds(0, z.tp - 1)], p_recv)
    sums = pout[...]
    for source in partners:
        sums += pin[source]
    gate, up, d_hidden = (sums[:, m * z.both:(m + 1) * z.both] for m in range(3))
    sig = jax.nn.sigmoid(gate)
    active = gate * sig
    hh[...] = (active * up).astype(BF16)
    hgu[:, :z.both] = (d_hidden * up * sig * (1.0 + gate * (1.0 - sig))).astype(BF16)
    hgu[:, z.both:] = (d_hidden * active).astype(BF16)

    def output(p):
        cols = pl.ds(p * z.piece, z.piece)
        out = jnp.dot(hh[...], wb[2, :, :, cols].reshape(-1, z.piece), preferred_element_type=F32)
        back = jnp.dot(hgu[...], wb[:2, :, :, cols].reshape(-1, z.piece), preferred_element_type=F32)
        for q in range(z.nch):
            for a, value in enumerate((out, back)):
                at = (2 * q + a) * z.rows
                ob[at:at + z.rows] = value[:, q * z.cw:(q + 1) * z.cw].astype(BF16)
        total = jnp.dot(perm_t[...], ob[...], preferred_element_type=F32)
        y[:, p] = total.astype(BF16).reshape(z.ep, z.xr, z.cw)
        for to in peers:
            send(y.at[to, p], yin.at[i, p], y_send, y_recv.at[p], (to, e, s))

    first = (((0,), (0,)), ((), ()))
    output(0)
    for t in range(z.tp):
        at = slice(t * z.hid, (t + 1) * z.hid)
        hs[t, 0] = hgu[:, at]
        hs[t, 1] = hgu[:, z.both + t * z.hid:z.both + (t + 1) * z.hid]
        hs[t, 2] = hh[:, at]
    packed = jnp.zeros((z.hid, z.lanes), F32)
    for m in range(3):
        packed += lax.dot_general(
            hs[s, m], place[m * z.rows:(m + 1) * z.rows], first, preferred_element_type=F32
        )
    lb[0] = packed.astype(BF16)
    upward = (2 * e) // z.edp
    for k in range(z.edp - 1):
        low = k + (k - e + z.edp) // z.edp
        high = z.edp - 1 - k
        high = high - (e - high + z.edp) // z.edp
        to = upward * low + (1 - upward) * high
        slot_at = lax.rem(e - to + z.edp, z.edp)
        send(lb.at[0], lb.at[slot_at], l_send, l_recv.at[slot_at], (i, to, s))
    for p in range(1, z.npc):
        output(p)
    yin[i] = y[i]

    @pl.when(s == owner)
    def _():
        for p in range(z.sub):
            rb[0, :, p] = xin[:, mine * z.sub + p]
        rb[1:, i] = zb[:, i // PARTS]
        for to in peers:
            landed(rb.at[others, to], r_recv.at[to])
            for k, core in enumerate(partners):
                send(rb.at[others, to], rb.at[others, to], q_send.at[k], q_recv, (i, e, core))

    @pl.when(s != owner)
    def _():
        landed(rb, q_recv)

    for r in range(z.edp):
        for p in range(z.sub):
            flat = jnp.dot(
                factor[...], rb[r, :, p].reshape(z.ep * z.xr, z.cw), preferred_element_type=F32
            ).astype(BF16)
            for q in range(z.nch):
                right[pl.ds(r * z.lanes, z.lanes), pl.ds(p * z.piece + q * z.cw, z.cw)] = flat[
                    q * z.lanes:(q + 1) * z.lanes
                ]
    for d in range(1, z.edp):
        landed(lb.at[d], l_recv.at[d])
    lane = lax.broadcasted_iota(jnp.int32, (1, z.lanes), 1)
    width = z.ep * CAP
    for m in range(3):
        keep = ((lane >= m * width) & (lane < (m + 1) * width)).astype(F32).astype(BF16)
        factors = jnp.concatenate([lb[r] * keep for r in range(z.edp)], axis=1)
        wg[m] = jnp.dot(factors, right[...], preferred_element_type=F32)

    for p in range(z.npc):
        landed(yin.at[pl.ds(0, z.ep - 1), p], y_recv.at[p])
        for w in range(z.window):
            total = yin[w * PARTS, p].astype(F32)
            for h in range(1, PARTS):
                total += yin[w * PARTS + h, p].astype(F32)
            summed[w, p] = (total * scales[w][1]).astype(BF16)

    landed(wb.at[:, pl.ds(0, z.tp - 1)], w_send)
    landed(xin.at[pl.ds(0, z.ep - 1)], x_send)
    landed(yin.at[pl.ds(0, z.ep - 1)], y_send)
    landed(pin.at[pl.ds(0, z.tp - 1)], p_send)
    landed(lb.at[others], l_send)

    @pl.when(s == owner)
    def _():
        if z.nblk > 1:
            landed(x.at[:, pl.ds(0, (z.nblk - 1) * z.sub)], z_send)
        landed(rb.at[others, pl.ds(0, z.ep - 1)], r_send)
        for k in range(z.tp - 1):
            landed(rb, q_send.at[k])

    @pl.when(s != owner)
    def _():
        landed(x, z_send)


def finish(z, wg, summed, homes, mixed, grad_tok, wgrad, mix, grad, sem):
    copies = []
    for m in range(3):
        copies.append(pltpu.make_async_copy(wg.at[m], wgrad.at[m], sem.at[m]))
        copies[-1].start()
    for p in range(z.npc):
        value = jnp.zeros((2 * z.nch * z.tok_rows, z.cw), F32)
        for w in range(z.window):
            home = homes[w].reshape(2 * z.nch * z.tok_rows, z.xr)
            value += jnp.dot(home, summed[w, p], preferred_element_type=F32)
        for q in range(z.nch):
            cols = pl.ds(p * z.piece + q * z.cw, z.cw)
            for a, target in ((0, mix), (1, grad)):
                at = (2 * q + a) * z.tok_rows
                target[:, cols] = value[at:at + z.tok_rows].astype(BF16)
    for a, target in ((0, mix), (1, grad)):
        copies.append(pltpu.make_async_copy(target, (mixed, grad_tok)[a], sem.at[3 + a]))
        copies[-1].start()
    for copy in copies:
        copy.wait()


def shards(tokens, cotangent, expert_ids, route_weights, expert_weights):
    z = Sizes(
        lax.axis_size("ep"), lax.axis_size("edp"), lax.axis_size("tp"),
        tokens.shape[0], tokens.shape[1], expert_weights.shape[1],
    )
    tables = jnp.asarray(permutations(z), BF16)
    operands = [tokens, cotangent, expert_ids.T, route_weights.T, tables, expert_weights]
    hbm = pl.BlockSpec(memory_space=pltpu.HBM)
    vmem = pl.BlockSpec(memory_space=pltpu.VMEM)
    dma = pltpu.SemaphoreType.DMA
    passed = pl.pallas_call(
        functools.partial(kernel, z),
        out_shape=(
            pltpu.VMEM((3, z.hid, z.block), F32),
            pltpu.VMEM((z.window, z.npc, z.xr, z.cw), BF16),
            pltpu.VMEM((z.window, 2 * z.nch, z.tok_rows, z.xr), BF16),
        ),
        in_specs=[hbm] * len(operands),
        out_specs=(vmem,) * 3,
        scratch_shapes=[
            pltpu.VMEM((2, *tokens.shape), BF16),
            *(pltpu.VMEM(o.shape, o.dtype) for o in operands[2:5]),
            pltpu.VMEM((3, z.tp, z.hid, z.feats), BF16),
            pltpu.VMEM((z.window, z.npc, z.xr, z.cw), BF16),
            pltpu.VMEM((z.ep, z.npc, z.xr, z.cw), BF16),
            pltpu.VMEM((z.edp - 1, z.window, z.sub, z.xr, z.cw), BF16),
            pltpu.VMEM((z.edp, z.ep, z.sub, z.xr, z.cw), BF16),
            pltpu.VMEM((2 * z.rows, z.piece), BF16),
            pltpu.VMEM((z.rows, 3 * z.both), F32),
            pltpu.VMEM((z.tp, z.rows, 3 * z.both), F32),
            pltpu.VMEM((z.rows, 2 * z.both), BF16),
            pltpu.VMEM((z.rows, z.both), BF16),
            pltpu.VMEM((z.tp, 3, z.rows, z.hid), BF16),
            pltpu.VMEM((z.edp, z.hid, z.lanes), BF16),
            pltpu.VMEM((z.nch * 2 * z.rows, z.cw), BF16),
            pltpu.VMEM((z.ep, z.npc, z.xr, z.cw), BF16),
            pltpu.VMEM((z.ep, z.npc, z.xr, z.cw), BF16),
            pltpu.VMEM((z.edp * z.lanes, z.block), BF16),
            dma((4,)), dma, dma, dma((z.nblk,)), dma, dma((z.npc,)), dma, dma, dma, dma((z.ep,)), dma, dma,
            dma, dma((z.edp,)), dma, dma((z.npc,)), dma((z.tp - 1,)), dma,
            pltpu.SemaphoreType.REGULAR((z.ep,)), pltpu.SemaphoreType.REGULAR, pltpu.SemaphoreType.REGULAR,
        ],
        compiler_params=pltpu.CompilerParams(
            collective_id=0, has_side_effects=True, vmem_limit_bytes=VMEM_LIMIT
        ),
        name="expert_block",
    )(*[pltpu.with_memory_space_constraint(o, pltpu.HBM) for o in operands])
    return pl.pallas_call(
        functools.partial(finish, z),
        out_shape=(
            jax.ShapeDtypeStruct(tokens.shape, BF16),
            jax.ShapeDtypeStruct(tokens.shape, BF16),
            jax.ShapeDtypeStruct((3, z.hid, z.block), F32),
        ),
        in_specs=[vmem] * 3,
        out_specs=(hbm,) * 3,
        scratch_shapes=[
            pltpu.VMEM(tokens.shape, BF16),
            pltpu.VMEM(tokens.shape, BF16),
            dma((5,)),
        ],
        compiler_params=pltpu.CompilerParams(vmem_limit_bytes=VMEM_LIMIT),
        name="finish",
    )(*[pltpu.with_memory_space_constraint(o, pltpu.VMEM) for o in passed])


def solution(mesh):
    placed = (
        P(("ep", "edp"), "tp"),
        P(("ep", "edp"), "tp"),
        P(("ep", "edp"), None),
        P(("ep", "edp"), None),
        P(None, ("ep", "tp"), None),
    )
    return jax.shard_map(
        shards,
        mesh=mesh,
        in_specs=placed,
        out_specs=(P(("ep", "edp"), "tp"), P(("ep", "edp"), "tp"), P(None, ("ep", "tp"), "edp")),
        check_vma=False,
    )
```

time: 24.6 us -> 23.1 us (0.939)
  Pallas kernels: 23.5 us -> 22 us
    pallas_call x1, Pallas kernels: 21.7 us -> 20.2 us  [shards(): pl.pallas_call(functools.partial(kernel, z), out_shape=(pltpu.VMEM((3, z....]
where the time goes in v2:
time: 23.1 us; the launch traced here: 22.6 us
  Pallas kernels  22 us (95%)
  between operations  0.64 us (3%)
    pallas_call x1, Pallas kernels, shards(): pl.pallas_call(functools.partial(kernel, z), out_shape=(pltpu.VMEM((3, z....  20.2 us
    pallas_call x1, Pallas kernels, shards(): pl.pallas_call(functools.partial(finish, z), out_shape=(jax.ShapeDtypeStr...  1.79 us

profile of v2, /device:TPU:1, one launch (start us, length us, event | category | flops | bytes accessed | tf_op | source)
XLA Modules:
  0.0 22.6 jit_solution(11776830290694229340)
XLA Ops:
  0.6 20.2 %expert_block.1 = (f32[3,192,1024]{2,1,0:T(8,128)S(1)}, bf16[1,4,40,256]{3,2,1,0:T(8,128)(2,1)S(1)}, bf16[1,4,128,40]{3,2,1,0:T(8,128)(2,1)S(1)}) custom-call(bf16[128,2048]{1,0:T(8,128)(2,1)} %tok_in.1, bf16[128,2048]{1,0:T(8,128)(2,1)} %cot_in.1, s32[8,128]{1,0:T(8,128)} %bitcast.2, f32[8,128]{1,0:T(8,128)} %bitcast.3, ...), custom_call_target="tpu_custom_call" | custom-call | tf_op jit(solution)/shard_map/expert_block/pallas_call | solution.py:424
  20.8 1.8 %finish.1 = (bf16[128,2048]{1,0:T(8,128)(2,1)}, bf16[128,2048]{1,0:T(8,128)(2,1)}, f32[3,192,1024]{2,1,0:T(8,128)}) custom-call(f32[3,192,1024]{2,1,0:T(8,128)S(1)} %get-tuple-element.6.wg, bf16[1,4,40,256]{3,2,1,0:T(8,128)(2,1)S(1)} %get-tuple-element.7.summed, bf16[1,4,128,40]{3,2,1,0:T(8,128)(2,1)S(1)} %get-tuple-element.8.homes), custom_call_target="tpu_custom_call" | custom-call | tf_op jit(solution)/shard_map/finish/pallas_call | solution.py:461

commit v3 on v2

--- a/solution.py
+++ b/solution.py
@@ -87,9 +87,9 @@
     z, tok_in, cot_in, ids_in, rw_in, tables_in, weights,
     wg, summed, homes,
     data, ids, rw, tables,
-    wb, x, xin, zb, rb, rows, pout, pin, hgu, hh, hs, lb, ob, y, yin, right,
+    wb, x, xin, zb, rb, rows, pout, pwire, pin, hgu, hh, hs, lb, ob, y, yin, right,
     in_sem, w_loc, w_send, w_recv, x_send, x_recv, z_send, z_recv, r_send, r_recv, p_send, p_recv,
-    l_send, l_recv, y_send, y_recv, q_send, q_recv, ep_ready, edp_ready, tp_ready,
+    l_send, l_recv, y_send, y_recv, q_send, q_recv, core_ready, plane_ready, edp_ready,
 ):
     i, e, s = lax.axis_index("ep"), lax.axis_index("edp"), lax.axis_index("tp")
     barrier = pltpu.get_barrier_semaphore()
@@ -103,38 +103,70 @@
     loads = [
         pltpu.make_async_copy(ids_in, ids, in_sem.at[0]),
         pltpu.make_async_copy(rw_in, rw, in_sem.at[1]),
-        pltpu.make_async_copy(tok_in, data.at[0], in_sem.at[2]),
-        pltpu.make_async_copy(cot_in, data.at[1], in_sem.at[2]),
     ]
+    head, rest = pl.ds(0, z.piece), pl.ds(z.piece, z.feats - z.piece)
+    for k, cols in enumerate((head, rest)):
+        loads.append(pltpu.make_async_copy(tok_in.at[:, cols], data.at[0, :, cols], in_sem.at[2 + k]))
+        loads.append(pltpu.make_async_copy(cot_in.at[:, cols], data.at[1, :, cols], in_sem.at[2 + k]))
     for copy in loads:
         copy.start()
 
-    def signal(semaphore, condition, to):
-        @pl.when(condition)
+    def signal(semaphore, to):
+        pl.semaphore_signal(semaphore, inc=1, device_id=to, device_id_type=MESH)
+
+    last_core = z.tp - 1
+    lead = s == last_core
+    @pl.when(lead)
+    def _():
+        for t in range(last_core):
+            signal(barrier, (i, e, t))
+
+    for to in peers:
+        signal(barrier, (to, e, last_core))
+    for d in range(1, z.edp):
+        @pl.when(e + d < z.edp)
         def _():
-            pl.semaphore_signal(semaphore, inc=1, device_id=to, device_id_type=MESH)
-
-    for to in partners:
-        signal(barrier, to > s, (i, e, to))
-    for to in peers:
-        signal(barrier, to > i, (to, e, s))
-    for d in range(1, z.edp):
-        signal(barrier, e + d < z.edp, (i, lax.rem(e + d, z.edp), s))
-
-    @pl.when(i + e + s > 0)
-    def _():
-        pl.semaphore_wait(barrier, i + e + s)
-
-    for to in partners:
-        signal(tp_ready, to < s, (i, e, to))
-    for to in peers:
-        signal(ep_ready.at[i], to < i, (to, e, s))
-    for d in range(1, z.edp):
-        signal(edp_ready, e - d >= 0, (i, lax.rem(e - d + z.edp, z.edp), s))
-
-    @pl.when(s < z.tp - 1)
-    def _():
-        pl.semaphore_wait(tp_ready, z.tp - 1 - s)
+            signal(barrier, (i, lax.rem(e + d, z.edp), 0))
+
+    @pl.when(s == 0)
+    def _():
+        pl.semaphore_wait(barrier, 1 + e * z.tp)
+
+    @pl.when((s != 0) & (s != last_core))
+    def _():
+        pl.semaphore_wait(barrier, 1)
+
+    @pl.when(s != last_core)
+    def _():
+        signal(core_ready, (i, e, last_core))
+        if z.tp > 2:
+            pl.semaphore_wait(core_ready, 1)
+
+    @pl.when(lead)
+    def _():
+        pl.semaphore_wait(core_ready, last_core)
+        if z.tp > 2:
+            for t in range(last_core):
+                signal(core_ready, (i, e, t))
+
+    @pl.when(s == 0)
+    def _():
+        for d in range(1, z.edp):
+            @pl.when(e - d >= 0)
+            def _():
+                for t in range(z.tp):
+                    signal(edp_ready, (i, lax.rem(e - d + z.edp, z.edp), t))
+
+    def enter():
+        @pl.when(lead)
+        def _():
+            pl.semaphore_wait(barrier, (z.ep - 1) * z.tp)
+            for t in range(last_core):
+                signal(plane_ready, (i, e, t))
+
+        @pl.when(s != last_core)
+        def _():
+            pl.semaphore_wait(plane_ready, 1)
 
     def send(source, target, send_sem, recv_sem, to):
         pltpu.make_async_remote_copy(
@@ -180,13 +212,11 @@
             [jnp.where((chunk == q) & (array == a), pick, 0.0).astype(BF16) for a in range(2)]
             for q in range(z.nch)
         ])
-    landed(data, in_sem.at[2])
+    landed(data.at[:, :, head], in_sem.at[2])
     own_w = pltpu.make_async_copy(
         weights.at[:, :, pl.ds(pl.multiple_of(s * z.feats, 128), z.feats)], wb.at[:, s], w_loc
     )
-    own_w.start()
-    table_load = pltpu.make_async_copy(tables_in, tables, in_sem.at[3])
-    table_load.start()
+    table_load = pltpu.make_async_copy(tables_in, tables, in_sem.at[4])
 
     def send_rows(p, to):
         send(x.at[to // PARTS, p], xin.at[i, p], x_send, x_recv.at[p], (to, e, s))
@@ -197,6 +227,10 @@
         send(x.at[:, pl.ds(b * z.sub, z.sub)], zb.at[slot_at], z_send, z_recv, (i, to, s))
 
     for p in range(z.npc):
+        if p == 1:
+            landed(data.at[:, :, rest], in_sem.at[3])
+            own_w.start()
+            table_load.start()
         for w in range(z.window):
             total = jnp.zeros((z.xr, z.cw), F32)
             for q in range(z.nch):
@@ -204,20 +238,23 @@
                 for a in range(2):
                     total += jnp.dot(chosen[w][q][a], data[a, :, cols], preferred_element_type=F32)
             x[w, p] = (total * scales[w][0]).astype(BF16)
-        for to in peers:
-            @pl.when(to < i)
+        if p % z.sub == z.sub - 1:
+            @pl.when(s * z.nblk + p // z.sub < e)
             def _():
+                send_replica(p // z.sub)
+
+    enter()
+
+    def send_all():
+        for p in range(z.npc):
+            for to in peers:
                 send_rows(p, to)
-    for to in reversed(peers):
-        @pl.when(to > i)
-        def _():
-            pl.semaphore_wait(ep_ready.at[to], 1)
-            for p in range(z.npc):
-                send_rows(p, to)
-    for b in range(z.nblk):
-        @pl.when(s * z.nblk + b < e)
-        def _():
-            send_replica(b)
+
+    early = lax.rem(s, 2) == 0
+
+    @pl.when(early)
+    def _():
+        send_all()
 
     for p in range(z.npc):
         xin[i, p] = x[i // PARTS, p]
@@ -228,63 +265,97 @@
                 homes[w, 2 * q + a] = jnp.where(
                     (lane_chunk == q) & (lane_array == a), home, 0.0
                 ).astype(BF16)
+
+    @pl.when(~early)
+    def _():
+        send_all()
+
+    @pl.when(e < z.edp - 1)
+    def _():
+        pl.semaphore_wait(edp_ready, z.edp - 1 - e)
+
+    for b in range(z.nblk):
+        @pl.when(s * z.nblk + b > e)
+        def _():
+            send_replica(b)
     own_w.wait()
     table_load.wait()
 
     owner = e // z.nblk
     mine = e - owner * z.nblk
     last = (((1,), (1,)), ((), ()))
-    for p in range(z.npc):
-        landed(xin.at[pl.ds(0, z.ep - 1), p], x_recv.at[p])
-        if p == 0:
-            @pl.when(e < z.edp - 1)
-            def _():
-                pl.semaphore_wait(edp_ready, z.edp - 1 - e)
-
-            for b in range(z.nblk):
-                @pl.when(s * z.nblk + b > e)
-                def _():
-                    send_replica(b)
+
+    def unpack(p):
         flat = jnp.dot(
             perm[...], xin[:, p].reshape(z.ep * z.xr, z.cw), preferred_element_type=F32
         ).astype(BF16)
         for q in range(z.nch):
-            rows[:, q * z.cw:(q + 1) * z.cw] = flat[q * 2 * z.rows:(q + 1) * 2 * z.rows]
+            rows[p % 2, :, q * z.cw:(q + 1) * z.cw] = flat[q * 2 * z.rows:(q + 1) * 2 * z.rows]
+
+    def wait_piece(p):
+        landed(xin.at[pl.ds(0, z.ep - 1), p], x_recv.at[p])
+
+    def wait_weights(p):
         if p % z.sub == 0:
             b = p // z.sub
             landed(wb.at[:, pl.ds(0, z.tp - 1), :, pl.ds(b * z.block, z.block)], w_recv.at[b])
+
+    def project(p):
         cols = pl.ds(p * z.piece, z.piece)
         first_two = lax.dot_general(
-            rows[:z.rows], wb[:2, :, :, cols].reshape(-1, z.piece), last, preferred_element_type=F32
+            rows[p % 2, :z.rows], wb[:2, :, :, cols].reshape(-1, z.piece), last, preferred_element_type=F32
         )
         third = lax.dot_general(
-            rows[z.rows:], wb[2, :, :, cols].reshape(-1, z.piece), last, preferred_element_type=F32
+            rows[p % 2, z.rows:], wb[2, :, :, cols].reshape(-1, z.piece), last, preferred_element_type=F32
         )
         if p:
             first_two += pout[:, :2 * z.both]
             third += pout[:, 2 * z.both:]
         pout[:, :2 * z.both] = first_two
         pout[:, 2 * z.both:] = third
+        if p == z.npc - 1:
+            pwire[:, :2 * z.both] = first_two.astype(BF16)
+            pwire[:, 2 * z.both:] = third.astype(BF16)
+
+    wait_piece(0)
+    unpack(0)
+    others = pl.ds(1, z.edp - 1)
+
+    def spread():
+        @pl.when(s == owner)
+        def _():
+            landed(zb, z_recv)
+            for to in peers:
+                send(zb.at[:, to // PARTS], rb.at[others, i], r_send, r_recv.at[i], (to, e, s))
+            for k, to in enumerate(partners):
+                send(zb.at[:, i // PARTS], rb.at[others, i], q_send.at[k], q_recv, (i, e, to))
+
+    for p in range(1, z.npc):
+        if p == 2:
+            spread()
+        if p < z.npc - 1:
+            wait_piece(p)
+        wait_weights(p - 1)
+        if p < z.npc - 1:
+            unpack(p)
+        project(p - 1)
+    wait_piece(z.npc - 1)
+    wait_weights(z.npc - 1)
+    unpack(z.npc - 1)
+    project(z.npc - 1)
     for to in partners:
-        send(pout, pin.at[s], p_send, p_recv, (i, e, to))
-
-    others = pl.ds(1, z.edp - 1)
+        send(pwire, pin.at[s], p_send, p_recv, (i, e, to))
 
     @pl.when(s == owner)
     def _():
-        landed(zb, z_recv)
-        for to in peers:
-            send(zb.at[:, to // PARTS], rb.at[others, i], r_send, r_recv.at[i], (to, e, s))
         for k, to in enumerate(partners):
-            send(
-                xin.at[:, pl.ds(mine * z.sub, z.sub)], rb.at[0], q_send.at[k], q_recv, (i, e, to),
-            )
-            send(zb.at[:, i // PARTS], rb.at[others, i], q_send.at[k], q_recv, (i, e, to))
+            send(xin.at[:, pl.ds(mine * z.sub, z.sub)], rb.at[0], q_send.at[k], q_recv, (i, e, to))
+
 
     landed(pin.at[pl.ds(0, z.tp - 1)], p_recv)
     sums = pout[...]
     for source in partners:
-        sums += pin[source]
+        sums += pin[source].astype(F32)
     gate, up, d_hidden = (sums[:, m * z.both:(m + 1) * z.both] for m in range(3))
     sig = jax.nn.sigmoid(gate)
     active = gate * sig
@@ -306,26 +377,30 @@
             send(y.at[to, p], yin.at[i, p], y_send, y_recv.at[p], (to, e, s))
 
     first = (((0,), (0,)), ((), ()))
+    def factors_out():
+        for t in range(z.tp):
+            at = slice(t * z.hid, (t + 1) * z.hid)
+            hs[t, :z.rows] = hgu[:, at]
+            hs[t, z.rows:2 * z.rows] = hgu[:, z.both + t * z.hid:z.both + (t + 1) * z.hid]
+            hs[t, 2 * z.rows:] = hh[:, at]
+        lb[0] = lax.dot_general(hs[s], place[...], first, preferred_element_type=F32).astype(BF16)
+        upward = (2 * e) // z.edp
+        for k in range(z.edp - 1):
+            low = k + (k - e + z.edp) // z.edp
+            high = z.edp - 1 - k
+            high = high - (e - high + z.edp) // z.edp
+            to = upward * low + (1 - upward) * high
+            slot_at = lax.rem(e - to + z.edp, z.edp)
+            send(lb.at[0], lb.at[slot_at], l_send, l_recv.at[slot_at], (i, to, s))
+
+    factors_first = (2 * e) // z.edp + lax.rem(s, 2) > 0
+    @pl.when(factors_first)
+    def _():
+        factors_out()
     output(0)
-    for t in range(z.tp):
-        at = slice(t * z.hid, (t + 1) * z.hid)
-        hs[t, 0] = hgu[:, at]
-        hs[t, 1] = hgu[:, z.both + t * z.hid:z.both + (t + 1) * z.hid]
-        hs[t, 2] = hh[:, at]
-    packed = jnp.zeros((z.hid, z.lanes), F32)
-    for m in range(3):
-        packed += lax.dot_general(
-            hs[s, m], place[m * z.rows:(m + 1) * z.rows], first, preferred_element_type=F32
-        )
-    lb[0] = packed.astype(BF16)
-    upward = (2 * e) // z.edp
-    for k in range(z.edp - 1):
-        low = k + (k - e + z.edp) // z.edp
-        high = z.edp - 1 - k
-        high = high - (e - high + z.edp) // z.edp
-        to = upward * low + (1 - upward) * high
-        slot_at = lax.rem(e - to + z.edp, z.edp)
-        send(lb.at[0], lb.at[slot_at], l_send, l_recv.at[slot_at], (i, to, s))
+    @pl.when(~factors_first)
+    def _():
+        factors_out()
     for p in range(1, z.npc):
         output(p)
     yin[i] = y[i]
@@ -353,14 +428,22 @@
                 right[pl.ds(r * z.lanes, z.lanes), pl.ds(p * z.piece + q * z.cw, z.cw)] = flat[
                     q * z.lanes:(q + 1) * z.lanes
                 ]
-    for d in range(1, z.edp):
-        landed(lb.at[d], l_recv.at[d])
     lane = lax.broadcasted_iota(jnp.int32, (1, z.lanes), 1)
     width = z.ep * CAP
-    for m in range(3):
-        keep = ((lane >= m * width) & (lane < (m + 1) * width)).astype(F32).astype(BF16)
-        factors = jnp.concatenate([lb[r] * keep for r in range(z.edp)], axis=1)
-        wg[m] = jnp.dot(factors, right[...], preferred_element_type=F32)
+    keeps = [((lane >= m * width) & (lane < (m + 1) * width)).astype(F32).astype(BF16) for m in range(3)]
+    near = max(1, z.edp // 2)
+    for part in (range(near), range(near, z.edp)):
+        for d in part:
+            if d:
+                landed(lb.at[d], l_recv.at[d])
+        for m in range(3):
+            factors = jnp.concatenate([lb[d] * keeps[m] for d in part], axis=1)
+            value = jnp.dot(
+                factors, right[part.start * z.lanes:part.stop * z.lanes], preferred_element_type=F32
+            )
+            if part.start:
+                value += wg[m]
+            wg[m] = value
 
     for p in range(z.npc):
         landed(yin.at[pl.ds(0, z.ep - 1), p], y_recv.at[p])
@@ -438,20 +521,21 @@
             pltpu.VMEM((z.ep, z.npc, z.xr, z.cw), BF16),
             pltpu.VMEM((z.edp - 1, z.window, z.sub, z.xr, z.cw), BF16),
             pltpu.VMEM((z.edp, z.ep, z.sub, z.xr, z.cw), BF16),
-            pltpu.VMEM((2 * z.rows, z.piece), BF16),
+            pltpu.VMEM((2, 2 * z.rows, z.piece), BF16),
             pltpu.VMEM((z.rows, 3 * z.both), F32),
-            pltpu.VMEM((z.tp, z.rows, 3 * z.both), F32),
+            pltpu.VMEM((z.rows, 3 * z.both), BF16),
+            pltpu.VMEM((z.tp, z.rows, 3 * z.both), BF16),
             pltpu.VMEM((z.rows, 2 * z.both), BF16),
             pltpu.VMEM((z.rows, z.both), BF16),
-            pltpu.VMEM((z.tp, 3, z.rows, z.hid), BF16),
+            pltpu.VMEM((z.tp, 3 * z.rows, z.hid), BF16),
             pltpu.VMEM((z.edp, z.hid, z.lanes), BF16),
             pltpu.VMEM((z.nch * 2 * z.rows, z.cw), BF16),
             pltpu.VMEM((z.ep, z.npc, z.xr, z.cw), BF16),
             pltpu.VMEM((z.ep, z.npc, z.xr, z.cw), BF16),
             pltpu.VMEM((z.edp * z.lanes, z.block), BF16),
-            dma((4,)), dma, dma, dma((z.nblk,)), dma, dma((z.npc,)), dma, dma, dma, dma((z.ep,)), dma, dma,
+            dma((5,)), dma, dma, dma((z.nblk,)), dma, dma((z.npc,)), dma, dma, dma, dma((z.ep,)), dma, dma,
             dma, dma((z.edp,)), dma, dma((z.npc,)), dma((z.tp - 1,)), dma,
-            pltpu.SemaphoreType.REGULAR((z.ep,)), pltpu.SemaphoreType.REGULAR, pltpu.SemaphoreType.REGULAR,
+            pltpu.SemaphoreType.REGULAR, pltpu.SemaphoreType.REGULAR, pltpu.SemaphoreType.REGULAR,
         ],
         compiler_params=pltpu.CompilerParams(
             collective_id=0, has_side_effects=True, vmem_limit_bytes=VMEM_LIMIT

time: 23.1 us -> 21.8 us (0.944); the launches traced: 22.6 us -> 21.6 us
  Pallas kernels: 22 us -> 20.9 us
    pallas_call x1, Pallas kernels: 20.2 us -> 19.1 us  [shards(): pl.pallas_call(functools.partial(kernel, z), out_shape=(pltpu.VMEM((3, z....]
where the time goes in v3:
time: 21.8 us; the launch traced here: 21.6 us
  Pallas kernels  20.9 us (96%)
  between operations  0.64 us (3%)
    pallas_call x1, Pallas kernels, shards(): pl.pallas_call(functools.partial(kernel, z), out_shape=(pltpu.VMEM((3, z....  19.1 us
    pallas_call x1, Pallas kernels, shards(): pl.pallas_call(functools.partial(finish, z), out_shape=(jax.ShapeDtypeStr...  1.79 us

profile of v3, /device:TPU:1, one launch (start us, length us, event | category | flops | bytes accessed | tf_op | source)
XLA Modules:
  0.0 21.6 jit_solution(11517348156763721075)
XLA Ops:
  0.6 19.1 %expert_block.1 = (f32[3,192,1024]{2,1,0:T(8,128)S(1)}, bf16[1,4,40,256]{3,2,1,0:T(8,128)(2,1)S(1)}, bf16[1,4,128,40]{3,2,1,0:T(8,128)(2,1)S(1)}) custom-call(bf16[128,2048]{1,0:T(8,128)(2,1)} %tok_in.1, bf16[128,2048]{1,0:T(8,128)(2,1)} %cot_in.1, s32[8,128]{1,0:T(8,128)} %bitcast.2, f32[8,128]{1,0:T(8,128)} %bitcast.3, ...), custom_call_target="tpu_custom_call" | custom-call | tf_op jit(solution)/shard_map/expert_block/pallas_call | solution.py:507
  19.8 1.8 %finish.1 = (bf16[128,2048]{1,0:T(8,128)(2,1)}, bf16[128,2048]{1,0:T(8,128)(2,1)}, f32[3,192,1024]{2,1,0:T(8,128)}) custom-call(f32[3,192,1024]{2,1,0:T(8,128)S(1)} %get-tuple-element.6.wg, bf16[1,4,40,256]{3,2,1,0:T(8,128)(2,1)S(1)} %get-tuple-element.7.summed, bf16[1,4,128,40]{3,2,1,0:T(8,128)(2,1)S(1)} %get-tuple-element.8.homes), custom_call_target="tpu_custom_call" | custom-call | tf_op jit(solution)/shard_map/finish/pallas_call | solution.py:545

commit v4 on v3

--- a/solution.py
+++ b/solution.py
@@ -326,7 +326,7 @@
         def _():
             landed(zb, z_recv)
             for to in peers:
-                send(zb.at[:, to // PARTS], rb.at[others, i], r_send, r_recv.at[i], (to, e, s))
+                send(zb.at[:, to // PARTS], rb.at[others, i], r_send, r_recv, (to, e, s))
             for k, to in enumerate(partners):
                 send(zb.at[:, i // PARTS], rb.at[others, i], q_send.at[k], q_recv, (i, e, to))
 
@@ -377,6 +377,8 @@
             send(y.at[to, p], yin.at[i, p], y_send, y_recv.at[p], (to, e, s))
 
     first = (((0,), (0,)), ((), ()))
+    near = max(1, (z.edp + 1) // 2)
+
     def factors_out():
         for t in range(z.tp):
             at = slice(t * z.hid, (t + 1) * z.hid)
@@ -391,7 +393,7 @@
             high = high - (e - high + z.edp) // z.edp
             to = upward * low + (1 - upward) * high
             slot_at = lax.rem(e - to + z.edp, z.edp)
-            send(lb.at[0], lb.at[slot_at], l_send, l_recv.at[slot_at], (i, to, s))
+            send(lb.at[0], lb.at[slot_at], l_send, l_recv.at[slot_at // near], (i, to, s))
 
     factors_first = (2 * e) // z.edp + lax.rem(s, 2) > 0
     @pl.when(factors_first)
@@ -410,8 +412,8 @@
         for p in range(z.sub):
             rb[0, :, p] = xin[:, mine * z.sub + p]
         rb[1:, i] = zb[:, i // PARTS]
+        landed(rb.at[others, pl.ds(0, z.ep - 1)], r_recv)
         for to in peers:
-            landed(rb.at[others, to], r_recv.at[to])
             for k, core in enumerate(partners):
                 send(rb.at[others, to], rb.at[others, to], q_send.at[k], q_recv, (i, e, core))
 
@@ -431,20 +433,21 @@
     lane = lax.broadcasted_iota(jnp.int32, (1, z.lanes), 1)
     width = z.ep * CAP
     keeps = [((lane >= m * width) & (lane < (m + 1) * width)).astype(F32).astype(BF16) for m in range(3)]
-    near = max(1, z.edp // 2)
-    for part in (range(near), range(near, z.edp)):
-        for d in part:
-            if d:
-                landed(lb.at[d], l_recv.at[d])
+    def weight_gradients(part):
+        start = max(1, part.start)
+        if part.stop > start:
+            landed(lb.at[pl.ds(start, part.stop - start)], l_recv.at[part.start // near])
+        factors = jnp.concatenate(
+            [jnp.concatenate([lb[d] * keeps[m] for d in part], axis=1) for m in range(3)], axis=0
+        )
+        value = jnp.dot(
+            factors, right[part.start * z.lanes:part.stop * z.lanes], preferred_element_type=F32
+        )
         for m in range(3):
-            factors = jnp.concatenate([lb[d] * keeps[m] for d in part], axis=1)
-            value = jnp.dot(
-                factors, right[part.start * z.lanes:part.stop * z.lanes], preferred_element_type=F32
-            )
-            if part.start:
-                value += wg[m]
-            wg[m] = value
-
+            rows_of = value[m * z.hid:(m + 1) * z.hid]
+            wg[m] = rows_of + wg[m] if part.start else rows_of
+
+    weight_gradients(range(near))
     for p in range(z.npc):
         landed(yin.at[pl.ds(0, z.ep - 1), p], y_recv.at[p])
         for w in range(z.window):
@@ -452,6 +455,8 @@
             for h in range(1, PARTS):
                 total += yin[w * PARTS + h, p].astype(F32)
             summed[w, p] = (total * scales[w][1]).astype(BF16)
+
+    weight_gradients(range(near, z.edp))
 
     landed(wb.at[:, pl.ds(0, z.tp - 1)], w_send)
     landed(xin.at[pl.ds(0, z.ep - 1)], x_send)
@@ -533,8 +538,8 @@
             pltpu.VMEM((z.ep, z.npc, z.xr, z.cw), BF16),
             pltpu.VMEM((z.ep, z.npc, z.xr, z.cw), BF16),
             pltpu.VMEM((z.edp * z.lanes, z.block), BF16),
-            dma((5,)), dma, dma, dma((z.nblk,)), dma, dma((z.npc,)), dma, dma, dma, dma((z.ep,)), dma, dma,
-            dma, dma((z.edp,)), dma, dma((z.npc,)), dma((z.tp - 1,)), dma,
+            dma((5,)), dma, dma, dma((z.nblk,)), dma, dma((z.npc,)), dma, dma, dma, dma, dma, dma,
+            dma, dma((2,)), dma, dma((z.npc,)), dma((z.tp - 1,)), dma,
             pltpu.SemaphoreType.REGULAR, pltpu.SemaphoreType.REGULAR, pltpu.SemaphoreType.REGULAR,
         ],
         compiler_params=pltpu.CompilerParams(

time: 21.8 us -> 21.6 us (level)
  no operation moved by 1% of the time
where the time goes in v4:
time: 21.6 us; the launch traced here: 21.4 us
  Pallas kernels  20.8 us (96%)
  between operations  0.64 us (3%)
    pallas_call x1, Pallas kernels, shards(): pl.pallas_call(functools.partial(kernel, z), out_shape=(pltpu.VMEM((3, z....  19 us
    pallas_call x1, Pallas kernels, shards(): pl.pallas_call(functools.partial(finish, z), out_shape=(jax.ShapeDtypeStr...  1.79 us

profile of v4, /device:TPU:1, one launch (start us, length us, event | category | flops | bytes accessed | tf_op | source)
XLA Modules:
  0.0 21.4 jit_solution(1378077534911938802)
XLA Ops:
  0.6 19.0 %expert_block.1 = (f32[3,192,1024]{2,1,0:T(8,128)S(1)}, bf16[1,4,40,256]{3,2,1,0:T(8,128)(2,1)S(1)}, bf16[1,4,128,40]{3,2,1,0:T(8,128)(2,1)S(1)}) custom-call(bf16[128,2048]{1,0:T(8,128)(2,1)} %tok_in.1, bf16[128,2048]{1,0:T(8,128)(2,1)} %cot_in.1, s32[8,128]{1,0:T(8,128)} %bitcast.2, f32[8,128]{1,0:T(8,128)} %bitcast.3, ...), custom_call_target="tpu_custom_call" | custom-call | tf_op jit(solution)/shard_map/expert_block/pallas_call | solution.py:512
  19.7 1.8 %finish.1 = (bf16[128,2048]{1,0:T(8,128)(2,1)}, bf16[128,2048]{1,0:T(8,128)(2,1)}, f32[3,192,1024]{2,1,0:T(8,128)}) custom-call(f32[3,192,1024]{2,1,0:T(8,128)S(1)} %get-tuple-element.6.wg, bf16[1,4,40,256]{3,2,1,0:T(8,128)(2,1)S(1)} %get-tuple-element.7.summed, bf16[1,4,128,40]{3,2,1,0:T(8,128)(2,1)S(1)} %get-tuple-element.8.homes), custom_call_target="tpu_custom_call" | custom-call | tf_op jit(solution)/shard_map/finish/pallas_call | solution.py:550

commit v5 on v3

--- a/solution.py
+++ b/solution.py
@@ -89,7 +89,7 @@
     data, ids, rw, tables,
     wb, x, xin, zb, rb, rows, pout, pwire, pin, hgu, hh, hs, lb, ob, y, yin, right,
     in_sem, w_loc, w_send, w_recv, x_send, x_recv, z_send, z_recv, r_send, r_recv, p_send, p_recv,
-    l_send, l_recv, y_send, y_recv, q_send, q_recv, core_ready, plane_ready, edp_ready,
+    l_send, l_recv, y_send, y_recv, q_send, q_recv, core_ready, plane_ready, edp_ready, turn,
 ):
     i, e, s = lax.axis_index("ep"), lax.axis_index("edp"), lax.axis_index("tp")
     barrier = pltpu.get_barrier_semaphore()
@@ -219,7 +219,7 @@
     table_load = pltpu.make_async_copy(tables_in, tables, in_sem.at[4])
 
     def send_rows(p, to):
-        send(x.at[to // PARTS, p], xin.at[i, p], x_send, x_recv.at[p], (to, e, s))
+        send(x.at[to // PARTS, p], xin.at[i, p], x_send.at[min(p, 1)], x_recv.at[p], (to, e, s))
 
     def send_replica(b):
         to = s * z.nblk + b
@@ -245,16 +245,27 @@
 
     enter()
 
-    def send_all():
-        for p in range(z.npc):
+    ahead = max(1, z.npc - 1)
+
+    def send_pieces(pieces):
+        for p in pieces:
             for to in peers:
                 send_rows(p, to)
 
-    early = lax.rem(s, 2) == 0
-
-    @pl.when(early)
-    def _():
-        send_all()
+    def first_piece_left():
+        landed(xin.at[pl.ds(0, z.ep - 1), 0], x_send.at[0])
+
+    second = lax.rem(s, 2) == 1
+    has_second = (~second) & (s + 1 < z.tp)
+    send_pieces(range(1))
+
+    @pl.when(~second)
+    def _():
+        send_pieces(range(1, z.npc))
+
+    @pl.when(second)
+    def _():
+        send_pieces(range(1, ahead))
 
     for p in range(z.npc):
         xin[i, p] = x[i // PARTS, p]
@@ -266,9 +277,15 @@
                     (lane_chunk == q) & (lane_array == a), home, 0.0
                 ).astype(BF16)
 
-    @pl.when(~early)
-    def _():
-        send_all()
+    @pl.when(has_second)
+    def _():
+        first_piece_left()
+        signal(turn, (i, e, s + 1))
+
+    @pl.when(second)
+    def _():
+        pl.semaphore_wait(turn, 1)
+        send_pieces(range(ahead, z.npc))
 
     @pl.when(e < z.edp - 1)
     def _():
@@ -326,7 +343,7 @@
         def _():
             landed(zb, z_recv)
             for to in peers:
-                send(zb.at[:, to // PARTS], rb.at[others, i], r_send, r_recv.at[i], (to, e, s))
+                send(zb.at[:, to // PARTS], rb.at[others, i], r_send, r_recv, (to, e, s))
             for k, to in enumerate(partners):
                 send(zb.at[:, i // PARTS], rb.at[others, i], q_send.at[k], q_recv, (i, e, to))
 
@@ -410,8 +427,8 @@
         for p in range(z.sub):
             rb[0, :, p] = xin[:, mine * z.sub + p]
         rb[1:, i] = zb[:, i // PARTS]
+        landed(rb.at[others, pl.ds(0, z.ep - 1)], r_recv)
         for to in peers:
-            landed(rb.at[others, to], r_recv.at[to])
             for k, core in enumerate(partners):
                 send(rb.at[others, to], rb.at[others, to], q_send.at[k], q_recv, (i, e, core))
 
@@ -454,7 +471,12 @@
             summed[w, p] = (total * scales[w][1]).astype(BF16)
 
     landed(wb.at[:, pl.ds(0, z.tp - 1)], w_send)
-    landed(xin.at[pl.ds(0, z.ep - 1)], x_send)
+    landed(xin.at[pl.ds(0, z.ep - 1), pl.ds(1, z.npc - 1)], x_send.at[1])
+
+    @pl.when(~has_second)
+    def _():
+        first_piece_left()
+
     landed(yin.at[pl.ds(0, z.ep - 1)], y_send)
     landed(pin.at[pl.ds(0, z.tp - 1)], p_send)
     landed(lb.at[others], l_send)
@@ -533,9 +555,9 @@
             pltpu.VMEM((z.ep, z.npc, z.xr, z.cw), BF16),
             pltpu.VMEM((z.ep, z.npc, z.xr, z.cw), BF16),
             pltpu.VMEM((z.edp * z.lanes, z.block), BF16),
-            dma((5,)), dma, dma, dma((z.nblk,)), dma, dma((z.npc,)), dma, dma, dma, dma((z.ep,)), dma, dma,
+            dma((5,)), dma, dma, dma((z.nblk,)), dma((2,)), dma((z.npc,)), dma, dma, dma, dma, dma, dma,
             dma, dma((z.edp,)), dma, dma((z.npc,)), dma((z.tp - 1,)), dma,
-            pltpu.SemaphoreType.REGULAR, pltpu.SemaphoreType.REGULAR, pltpu.SemaphoreType.REGULAR,
+            *[pltpu.SemaphoreType.REGULAR] * 4,
         ],
         compiler_params=pltpu.CompilerParams(
             collective_id=0, has_side_effects=True, vmem_limit_bytes=VMEM_LIMIT

time: 21.8 us -> 21.5 us (0.986)
  the two profiles are of different devices: /device:TPU:1 before, /device:TPU:0 now
where the time goes in v5:
time: 21.5 us; the launch traced here: 21.3 us
  Pallas kernels  20.7 us (96%)
  between operations  0.64 us (3%)
    pallas_call x1, Pallas kernels, shards(): pl.pallas_call(functools.partial(kernel, z), out_shape=(pltpu.VMEM((3, z....  18.9 us
    pallas_call x1, Pallas kernels, shards(): pl.pallas_call(functools.partial(finish, z), out_shape=(jax.ShapeDtypeStr...  1.79 us

profile of v5, /device:TPU:0, one launch (start us, length us, event | category | flops | bytes accessed | tf_op | source)
XLA Modules:
  0.0 21.3 jit_solution(10179210097980348468)
XLA Ops:
  0.6 18.9 %expert_block.1 = (f32[3,192,1024]{2,1,0:T(8,128)S(1)}, bf16[1,4,40,256]{3,2,1,0:T(8,128)(2,1)S(1)}, bf16[1,4,128,40]{3,2,1,0:T(8,128)(2,1)S(1)}) custom-call(bf16[128,2048]{1,0:T(8,128)(2,1)} %tok_in.1, bf16[128,2048]{1,0:T(8,128)(2,1)} %cot_in.1, s32[8,128]{1,0:T(8,128)} %bitcast.2, f32[8,128]{1,0:T(8,128)} %bitcast.3, ...), custom_call_target="tpu_custom_call" | custom-call | tf_op jit(solution)/shard_map/expert_block/pallas_call | solution.py:529
  19.5 1.8 %finish.1 = (bf16[128,2048]{1,0:T(8,128)(2,1)}, bf16[128,2048]{1,0:T(8,128)(2,1)}, f32[3,192,1024]{2,1,0:T(8,128)}) custom-call(f32[3,192,1024]{2,1,0:T(8,128)S(1)} %get-tuple-element.6.wg, bf16[1,4,40,256]{3,2,1,0:T(8,128)(2,1)S(1)} %get-tuple-element.7.summed, bf16[1,4,128,40]{3,2,1,0:T(8,128)(2,1)S(1)} %get-tuple-element.8.homes), custom_call_target="tpu_custom_call" | custom-call | tf_op jit(solution)/shard_map/finish/pallas_call | solution.py:567
